TPU v7x, 512 devices: a 4x2x32 block of a 4x8x32 slice. The times are simulated.
512 devices in a mesh: kgrp: 2 (over y), pw: 64 (over z, core), band: 4 (over x).
Axes of the slice: x: 4, y: 2, z: 32, core: 2. Of those that a mesh axis runs over, the one named last changes fastest.
The devices are a block of a 4x8x32 slice.
Arguments:
- waves: float32 [128, 4, 256, 256], P('band', 'kgrp', 'pw'), parts along dimension 1, as said below
- forward: float32 [128, 4, 256, 256], P('band', 'kgrp', 'pw'), parts along dimension 1, as said below
- backward: float32 [128, 4, 256, 256], P('band', 'kgrp', 'pw'), parts along dimension 1, as said below
- projectors: float32 [256, 2, 256, 256], P('kgrp', None, 'pw'), parts along dimension 0, as said below
- potential: float32 [256, 256], P('pw'), may hold values from 0.25 to 2
- strengths: float32 [128], replicated, may hold values from 0.5 to 4
- shifts: float32 [128], P('band'), may hold values from 0.5 to 2
Outputs:
- response: float32 [128, 4, 256, 256], P('band', 'kgrp', 'pw'), parts along dimension 1
- derivative: float32 [128, 4, 256, 256], P('band', 'kgrp', 'pw'), parts along dimension 1
There are 2 independent parts, one for each index of `kgrp`. A program takes and returns all parts, laid end to end along the dimension named above; an argument that names none is the same for every part. Nothing has to cross between parts.
Inputs may be any that keep to these rules, and one draw needn't show every extreme that they name: `waves`: real and imaginary parts of every band's coefficients are drawn independently at every grid point. `forward`: the margin of the slab's bands with these coefficients is an invertible matrix. `backward`: the margin of the slab's bands with these coefficients is an invertible matrix. `projectors`: real and imaginary parts of every projector are drawn independently at every grid point.
All inputs are finite; a program needn't handle non-finite values.
Results may differ from a plain program's by a relative error of at most 0.0003.
Values sent between devices are 32-bit elements; how exact they have to be, the bound alone decides.
A program may use at most 64 MiB of HBM per device.

v0:
```python
import functools
import math

import jax
import jax.numpy as jnp
from jax import lax
from jax.sharding import Mesh
from jax.sharding import PartitionSpec as P

ITERS = 2
PW = ("pw_0", "pw_1")


precise = lax.Precision.HIGHEST
string_step = 0.05
kinetic_scale = 4.0


def sent_together(arrays, axis, dim, along):
    both = jnp.concatenate(arrays, axis=along)
    out, at, finished = (lax.all_gather(both, axis, axis=dim, tiled=True), 0, [])
    for a in arrays:
        finished.append(lax.slice_in_dim(out, at, at + a.shape[along], axis=along))
        at += a.shape[along]
    return tuple(finished)


def by_axis(shard, axes):
    return functools.reduce(lax.psum, axes, shard)


def split_up(shard, dim, count):
    before, after = (shard.shape[:dim], shard.shape[dim + 1 :])
    return jnp.moveaxis(shard.reshape(*before, count, -1, *after), dim, 0)


def joined_along(pieces, dim):
    pieces = jnp.moveaxis(pieces, 0, dim)
    lengths = pieces.shape
    return pieces.reshape(*lengths[:dim], lengths[dim] * lengths[dim + 1], *lengths[dim + 2 :])


def moved_by_axis(pieces, axes, turns):
    lengths = [lax.axis_size(a) for a in axes]
    pieces = pieces.reshape(*lengths, *pieces.shape[1:])
    for k in turns:
        pieces = lax.all_to_all(pieces, axes[k], split_axis=k, concat_axis=k, tiled=True)
    return pieces.reshape(-1, *pieces.shape[len(axes) :])


def core_and_chips(shard, groups, turns, split_dim, concat_dim):
    count = lax.axis_size(groups[0]) * lax.axis_size(groups[1])
    pieces = split_up(shard, split_dim, count)
    return joined_along(moved_by_axis(pieces, groups, turns), concat_dim)


def margin(left_set, right_set):
    products = jnp.einsum("ixg,jyg->xyij", left_set, right_set, precision=precise)
    return jnp.stack([products[0, 0] + products[1, 1], products[0, 1] - products[1, 0]])


def combine(vectors, coeffs):
    table = jnp.stack([jnp.stack([coeffs[0], coeffs[1]]), jnp.stack([-coeffs[1], coeffs[0]])])
    return jnp.einsum("ixg,xyij->jyg", vectors, table, precision=precise)


def invert(matrix):
    real_part = matrix[0]
    imag_part = matrix[1]
    embedded = jnp.concatenate(
        [jnp.concatenate([real_part, -imag_part], 1), jnp.concatenate([imag_part, real_part], 1)], 0
    )
    normal = jnp.dot(embedded.T, embedded, precision=precise)
    lower_factor = jnp.linalg.cholesky(normal)
    middle = lax.linalg.triangular_solve(lower_factor, embedded.T, left_side=True, lower=True)
    inverse = lax.linalg.triangular_solve(
        lower_factor, middle, left_side=True, lower=True, transpose_a=True
    )
    count_rows = real_part.shape[0]
    return jnp.stack([inverse[:count_rows, :count_rows], inverse[count_rows:, :count_rows]])


def centred(index, length):
    shifted = (index + length // 2) % length - length // 2
    return shifted.astype(jnp.float32) / length


def dft_table(length, sign):
    index = jnp.arange(length, dtype=jnp.int32)
    phase = index[:, None] * index[None, :] % length
    angle = phase.astype(jnp.float32) * (2.0 * math.pi / length)
    cosine = jnp.cos(angle) / math.sqrt(length)
    sine = sign * jnp.sin(angle) / math.sqrt(length)
    return jnp.stack([jnp.stack([cosine, sine]), jnp.stack([-sine, cosine])])


def body(waves, forward, backward, projectors, potential, strengths, shifts):
    bands = waves.shape[0]
    rows = waves.shape[2]
    width = waves.shape[3]
    peers = lax.axis_size(PW)
    length = rows * peers
    points = float(length * width)
    cells = rows * width
    quarter = width // peers
    waves_flat = waves.reshape(bands, 2, cells)
    forward_flat = forward.reshape(bands, 2, cells)
    backward_flat = backward.reshape(bands, 2, cells)
    offset = lax.axis_index("band") * bands
    every_forward, every_backward = sent_together((forward_flat, backward_flat), "band", 0, 1)
    forward_part = margin(waves_flat, every_forward) / points
    backward_part = margin(waves_flat, every_backward) / points
    forward_part, backward_part = (by_axis(forward_part, PW), by_axis(backward_part, PW))
    forward_whole, backward_whole = sent_together((forward_part, backward_part), "band", 1, 0)
    forward_inverse = invert(forward_whole)
    backward_inverse = -invert(backward_whole)
    forward_cols = lax.dynamic_slice_in_dim(forward_inverse, offset, bands, 2)
    backward_cols = lax.dynamic_slice_in_dim(backward_inverse, offset, bands, 2)
    moved = combine(every_forward, forward_cols) + combine(every_backward, backward_cols)
    derivative = (moved / (2.0 * string_step)).reshape(bands, 2, rows, width)
    first_index = lax.axis_index(PW) * rows + jnp.arange(rows, dtype=jnp.int32)
    second_index = jnp.arange(width, dtype=jnp.int32)
    first_freq = centred(first_index, length)
    second_freq = centred(second_index, width)
    kinetic = kinetic_scale * (
        first_freq[:, None] * first_freq[:, None] + second_freq[None, :] * second_freq[None, :]
    )
    diagonal = kinetic[None, None] + shifts[:, None, None, None]
    width_out = dft_table(width, 1.0)
    width_back = dft_table(width, -1.0)
    long_out = dft_table(length, 1.0).reshape(2, 2, peers, rows, length)
    long_back = dft_table(length, -1.0).reshape(2, 2, length, peers, rows)
    projector_flat = projectors.reshape(projectors.shape[0], 2, cells)
    residual = -derivative
    direction = residual
    solution = jnp.zeros_like(residual)
    norm_now = by_axis(jnp.sum(residual * residual, axis=(1, 2, 3)), PW)
    for turn in range(ITERS):
        sectioned = jnp.einsum("bxrj,xyjk->ykrb", direction, width_out, precision=precise).reshape(
            2, width, rows * bands
        )
        arrived = lax.all_to_all(sectioned, PW, split_axis=1, concat_axis=2, tiled=True).reshape(
            2, quarter, peers, rows, bands
        )
        field = jnp.einsum("xqsrb,xysrk->yqbk", arrived, long_out, precision=precise)
        weighted = field * potential[None, :, None, :]
        leaving = jnp.einsum("xqbk,xyksr->yqsrb", weighted, long_back, precision=precise).reshape(
            2, quarter, peers * rows * bands
        )
        returned = core_and_chips(leaving, ("pw_0", "pw_1"), (1, 0), 2, 1).reshape(
            2, width, rows, bands
        )
        smooth_part = jnp.einsum("xkrb,xykj->byrj", returned, width_back, precision=precise)
        coupling = margin(projector_flat, direction.reshape(bands, 2, cells)) / points
        own_energy = jnp.sum(diagonal * direction * direction, axis=(1, 2, 3)) + jnp.sum(
            weighted * field, axis=(0, 1, 3)
        )
        coupling, own_energy = (by_axis(coupling, PW), by_axis(own_energy, PW))
        nonlocal_part = combine(projector_flat, coupling * strengths[None, :, None]).reshape(
            direction.shape
        )
        image = diagonal * direction + smooth_part + nonlocal_part
        curvature = own_energy + points * jnp.sum(
            strengths[None, :, None] * coupling * coupling, axis=(0, 1)
        )
        image, curvature = (image, curvature)
        alpha = (norm_now / curvature)[:, None, None, None]
        solution = solution + alpha * direction
        if turn + 1 < ITERS:
            residual = residual - alpha * image
            norm_next = by_axis(jnp.sum(residual * residual, axis=(1, 2, 3)), PW)
            direction = residual + (norm_next / norm_now)[:, None, None, None] * direction
            norm_now = norm_next
    return (solution, derivative)


def solution(mesh):
    split = Mesh(
        mesh.devices.reshape(mesh.shape["kgrp"], 32, 2, mesh.shape["band"]),
        ("kgrp", "pw_0", "pw_1", "band"),
    )
    return jax.shard_map(
        body,
        mesh=split,
        in_specs=(
            P("band", "kgrp", PW, None),
            P("band", "kgrp", PW, None),
            P("band", "kgrp", PW, None),
            P("kgrp", None, PW, None),
            P(PW, None),
            P(),
            P("band"),
        ),
        out_specs=(P("band", "kgrp", PW, None), P("band", "kgrp", PW, None)),
        check_vma=False,
    )
```

profile of v0, /device:TPU:33, one launch (start us, length us, event | category | flops | bytes accessed | tf_op | source)
XLA Modules:
  0.0 990.5 jit_solution(6514373329884496836)
XLA Ops:
  7.3 1.2 reshape.616
  8.5 1.2 reshape.617
  9.8 0.8 pad_maximum_fusion.4
  11.1 1.0 fusion.83
  12.1 1.1 cosine_multiply_fusion.1
  13.2 1.0 broadcast_multiply_fusion.1
  14.3 68.9 %all-gather.2.cloned.1.call-done = f32[128,4,1024]{2,0,1:T(8,128)} async-done(((f32[32,4,1024]{2,0,1:T(8,128)}), f32[128,4,1024]{2,0,1:T(8,128)}) %all-gather.2.cloned.1.call-update) | async-done | bytes 2097168 | tf_op jit(solution)/shard_map/all_gather | solution.py:21
  83.2 2.3 convolution_bitcast_fusion.11
  85.5 2.3 convolution_bitcast_fusion.10
  89.1 1.4 fusion.28
  90.6 226.8 %all-reduce.10.cloned.1.call-done = (f32[2,32,128]{2,1,0:T(8,128)}, f32[2,32,128]{2,1,0:T(8,128)}) async-done(((f32[2,32,128]{2,1,0:T(8,128)}, f32[2,32,128]{2,1,0:T(8,128)}), (f32[2,32,128]{2,1,0:T(8,128)}, f32[2,32,128]{2,1,0:T(8,128)})) %all-reduce.10.cloned.1.call-update) | async-done | bytes 65552 | tf_op jit(solution)/shard_map/psum | solution.py:29
  317.5 73.2 %all-reduce.12.cloned.1.call-done = (f32[2,32,128]{2,1,0:T(8,128)}, f32[2,32,128]{2,1,0:T(8,128)}) async-done(((f32[2,32,128]{2,1,0:T(8,128)}, f32[2,32,128]{2,1,0:T(8,128)}), (f32[2,32,128]{2,1,0:T(8,128)}, f32[2,32,128]{2,1,0:T(8,128)})) %all-reduce.12.cloned.1.call-update) | async-done | bytes 65552 | tf_op jit(solution)/shard_map/psum | solution.py:29
  390.6 0.8 pad_maximum_fusion.5
  391.4 9.6 all_gather.7
  401.8 11.7 %cholesky.130 = f32[128,128]{1,0:T(8,128)S(1)} custom-call(f32[128,128]{1,0:T(8,128)S(1)} %cholesky.194), custom_call_target="Cholesky" | custom-call | tf_op jit(solution)/shard_map/jit(cholesky)/cholesky | solution.py:74
  413.6 9.8 custom-call.17
  423.9 11.7 %cholesky.147 = f32[128,128]{1,0:T(8,128)S(1)} custom-call(f32[128,128]{1,0:T(8,128)S(1)} %convolution_subtract_fusion.3), custom_call_target="Cholesky" | custom-call | tf_op jit(solution)/shard_map/jit(cholesky)/cholesky | solution.py:74
  435.7 0.6 compare_reduce_fusion.2
  438.4 4.0 while.8
  439.0 1.4 bitcast_dynamic-update-slice_fusion.4
  441.0 1.4 bitcast_dynamic-update-slice_fusion.4
  442.4 19.9 %custom-call.19 = f32[2,128,128]{1,2,0:T(8,128)S(1)} custom-call(f32[2,128,128]{2,1,0:T(8,128)S(1)} %get-tuple-element.34), custom_call_target="InvertDiagBlocksLowerTriangular" | custom-call | tf_op jit(solution)/shard_map/triangular_solve/custom-call.4 | solution.py:76
  463.6 1.0 fusion.111
  465.4 11.7 %cholesky.164 = f32[128,128]{1,0:T(8,128)S(1)} custom-call(f32[128,128]{1,0:T(8,128)S(1)} %cholesky.197), custom_call_target="Cholesky" | custom-call | tf_op jit(solution)/shard_map/jit(cholesky)/cholesky | solution.py:74
  477.2 9.8 custom-call.20
  487.5 11.7 %cholesky.181 = f32[128,128]{1,0:T(8,128)S(1)} custom-call(f32[128,128]{1,0:T(8,128)S(1)} %convolution_subtract_fusion.2), custom_call_target="Cholesky" | custom-call | tf_op jit(solution)/shard_map/jit(cholesky)/cholesky | solution.py:74
  499.2 0.7 compare_reduce_fusion
  502.3 4.0 while.9
  503.0 1.4 bitcast_dynamic-update-slice_fusion.5
  505.0 1.4 bitcast_dynamic-update-slice_fusion.5
  506.3 19.7 %custom-call.22 = f32[2,128,128]{1,2,0:T(8,128)S(1)} custom-call(f32[2,128,128]{2,1,0:T(8,128)S(1)} %get-tuple-element.36), custom_call_target="InvertDiagBlocksLowerTriangular" | custom-call | tf_op jit(solution)/shard_map/triangular_solve/custom-call.4 | solution.py:76
  527.7 1.2 convolution_bitcast_fusion.7
  529.4 0.8 convolution_bitcast_fusion.1
  530.2 1.4 fusion.40
  531.6 1.9 fusion.25
  533.5 0.8 copy.217
  534.4 25.6 %all-to-all-start = ((f32[2,256,128]{2,0,1:T(2,128)}), f32[2,256,128]{2,0,1:T(2,128)S(1)}, u32[]{:S(2)}, u32[]{:S(2)}) async-start(f32[2,256,128]{2,0,1:T(2,128)} %copy.217), calls=%async_computation | async-start | bytes 524288 | tf_op jit(solution)/shard_map/all_to_all | solution.py:142
  560.0 0.9 reshape.526
  560.9 1.9 sine_multiply_fusion.1
  562.8 2.0 sine_multiply_fusion
  564.8 35.3 %all-to-all-done = f32[2,256,128]{2,0,1:T(2,128)S(1)} async-done(((f32[2,256,128]{2,0,1:T(2,128)}), f32[2,256,128]{2,0,1:T(2,128)S(1)}, u32[]{:S(2)}, u32[]{:S(2)}) %all-to-all-start) | async-done | bytes 262176 | tf_op jit(solution)/shard_map/all_to_all | solution.py:142
  600.4 2.6 fusion.39
  603.1 1.6 convolution_bitcast_fusion
  605.0 6.0 all_to_all.40
  611.0 0.9 copy.228
  611.9 4.8 all-to-all-start.2
  616.8 1.2 convolution_bitcast_fusion.9
  618.1 99.2 %all-reduce.2 = (f32[2,128,32]{1,2,0:T(8,128)S(1)}, f32[32]{0:T(128)S(1)}, f32[32]{0:T(128)S(1)}) all-reduce(f32[2,128,32]{1,2,0:T(8,128)S(1)} %maximum_multiply_fusion.2, f32[32]{0:T(128)S(1)} %get-tuple-element.50, f32[32]{0:T(128)S(1)} %add.353), channel_id=1, replica_groups=mesh['kgrp'=2,'pw_0'=32,'pw_1'=2,'band'=4] {'pw_0'}, use_global_device_ids=true, to_apply=%region_15.19 | all-reduce | flops 8256 | bytes 66048 | tf_op jit(solution)/shard_map/psum | solution.py:29
  717.3 29.3 %all-reduce.5 = (f32[2,128,32]{1,2,0:T(8,128)S(1)}, f32[32]{0:T(128)S(1)}, f32[32]{0:T(128)S(1)}) all-reduce(f32[2,128,32]{1,2,0:T(8,128)S(1)} %get-tuple-element.69, f32[32]{0:T(128)S(1)} %get-tuple-element.70, f32[32]{0:T(128)S(1)} %get-tuple-element.71), channel_id=1, replica_groups=mesh['kgrp'=2,'pw_0'=32,'pw_1'=2,'band'=4] {'pw_1'}, use_global_device_ids=true, to_apply=%region_16.20 | all-reduce | flops 8256 | bytes 66048 | tf_op jit(solution)/shard_map/psum | solution.py:29
  746.7 1.7 fusion.16
  749.3 1.0 copy.232
  750.3 2.2 multiply_reduce_fusion
  752.5 39.8 %psum.122 = f32[32]{0:T(128)S(1)} all-reduce(f32[32]{0:T(128)S(1)} %get-tuple-element.133), channel_id=1, replica_groups=mesh['kgrp'=2,'pw_0'=32,'pw_1'=2,'band'=4] {'pw_0'}, use_global_device_ids=true, to_apply=%region_19.23 | all-reduce | flops 32 | bytes 256 | tf_op jit(solution)/shard_map/psum | solution.py:29
  792.4 15.9 %psum.123 = f32[32]{0:T(128)S(1)} all-reduce(f32[32]{0:T(128)S(1)} %psum.122), channel_id=1, replica_groups=mesh['kgrp'=2,'pw_0'=32,'pw_1'=2,'band'=4] {'pw_1'}, use_global_device_ids=true, to_apply=%region_20.24 | all-reduce | flops 32 | bytes 256 | tf_op jit(solution)/shard_map/psum | solution.py:29
  808.5 0.7 fusion.24
  809.3 0.8 copy.236
  810.1 20.2 %all-to-all-start.3 = ((f32[2,256,128]{2,0,1:T(2,128)}), f32[2,256,128]{2,0,1:T(2,128)S(1)}, u32[]{:S(2)}, u32[]{:S(2)}) async-start(f32[2,256,128]{2,0,1:T(2,128)} %copy.236), calls=%async_computation.3 | async-start | bytes 524288 | tf_op jit(solution)/shard_map/all_to_all | solution.py:142
  830.5 0.7 copy.243
  831.2 1.2 convolution_bitcast_fusion.8
  832.4 39.1 %all-to-all-done.3 = f32[2,256,128]{2,0,1:T(2,128)S(1)} async-done(((f32[2,256,128]{2,0,1:T(2,128)}), f32[2,256,128]{2,0,1:T(2,128)S(1)}, u32[]{:S(2)}, u32[]{:S(2)}) %all-to-all-start.3) | async-done | bytes 262176 | tf_op jit(solution)/shard_map/all_to_all | solution.py:142
  871.8 0.9 fusion.36
  872.7 77.5 %all-reduce.1 = (f32[32]{0:T(128)S(1)}, f32[2,128,32]{1,2,0:T(8,128)S(1)}) all-reduce(f32[32]{0:T(128)S(1)} %add.364, f32[2,128,32]{1,2,0:T(8,128)S(1)} %maximum_multiply_fusion.3), channel_id=1, replica_groups=mesh['kgrp'=2,'pw_0'=32,'pw_1'=2,'band'=4] {'pw_0'}, use_global_device_ids=true, to_apply=%region_23.27 | all-reduce | flops 8224 | bytes 65792 | tf_op jit(solution)/shard_map/psum | solution.py:29
  950.2 32.5 %all-reduce.4 = (f32[32]{0:T(128)S(1)}, f32[2,128,32]{1,2,0:T(8,128)S(1)}) all-reduce(f32[32]{0:T(128)S(1)} %get-tuple-element.67, f32[2,128,32]{1,2,0:T(8,128)S(1)} %get-tuple-element.68), channel_id=1, replica_groups=mesh['kgrp'=2,'pw_0'=32,'pw_1'=2,'band'=4] {'pw_1'}, use_global_device_ids=true, to_apply=%region_24.28 | all-reduce | flops 8224 | bytes 65792 | tf_op jit(solution)/shard_map/psum | solution.py:29
  982.9 0.9 copy.242
  (147 shorter events, 14.5 us)
Async XLA Ops:
  7.2 3.6 copy-start.13
  7.2 76.0 %all-gather.2.cloned.1.call-start = ((), (), s32[]{:S(2)}) async-start(), calls=%async_computation.4 | async-start | bytes 2621440 | tf_op jit(solution)/shard_map/all_gather | solution.py:21
  9.7 4.5 copy-start.14
  10.7 306.7 %all-reduce.10.cloned.1.call-start = ((), (), s32[]{:S(2)}) async-start(), calls=%async_computation.5 | async-start | bytes 131072 | tf_op jit(solution)/shard_map/psum | solution.py:29
  89.1 301.6 %all-reduce.12.cloned.1.call-start = ((), (), s32[]{:S(2)}) async-start(), calls=%async_computation.6 | async-start | bytes 131072 | tf_op jit(solution)/shard_map/psum | solution.py:29
  462.3 2.9 copy-start.5
  463.6 38.7 %copy-start.4 = (f32[128,256]{1,0:T(8,128)}, f32[128,256]{1,0:T(8,128)S(1)}, u32[]{:S(2)}) copy-start(f32[128,256]{1,0:T(8,128)S(1)} %fusion.104) | copy-start | bytes 393220
  502.3 26.5 %slice-start = ((f32[128,256]{1,0:T(8,128)}), f32[128,128]{1,0:T(8,128)S(1)}, s32[]{:S(2)}) async-start(f32[128,256]{1,0:T(8,128)} %copy-done.4), calls=%async_computation.7 | async-start | bytes 131072 | tf_op jit(solution)/shard_map/slice | solution.py:80
  502.3 27.1 %copy-start.1 = (f32[128,4,1024]{2,0,1:T(8,128)S(1)}, f32[128,4,1024]{2,0,1:T(8,128)}, u32[]{:S(2)}) copy-start(f32[128,4,1024]{2,0,1:T(8,128)} %all-gather.2.cloned.1.call-done) | copy-start | bytes 6291460
  530.2 29.8 %copy-start = (f32[128,2,4,256]{3,2,1,0:T(4,128)S(1)}, f32[128,2,4,256]{3,2,1,0:T(4,128)}, u32[]{:S(2)}) copy-start(f32[128,2,4,256]{3,2,1,0:T(4,128)} %param.15) | copy-start | bytes 3145732
  534.4 65.8 %all-to-all-start = ((f32[2,256,128]{2,0,1:T(2,128)}), f32[2,256,128]{2,0,1:T(2,128)S(1)}, u32[]{:S(2)}, u32[]{:S(2)}) async-start(f32[2,256,128]{2,0,1:T(2,128)} %copy.217), calls=%async_computation | async-start | bytes 524288 | tf_op jit(solution)/shard_map/all_to_all | solution.py:142
  559.9 40.5 %copy-start.17 = (f32[4,256]{1,0:T(4,128)S(1)}, f32[4,256]{1,0:T(4,128)}, u32[]{:S(2)}) copy-start(f32[4,256]{1,0:T(4,128)} %param.16) | copy-start | bytes 12292
  562.8 40.2 %copy-start.6 = (f32[1,1,64,4,256]{4,2,0,3,1:T(8,128)}, f32[1,1,64,4,256]{4,2,0,3,1:T(8,128)S(1)}, u32[]{:S(2)}) copy-start(f32[1,1,64,4,256]{4,2,0,3,1:T(8,128)S(1)} %get-tuple-element.121) | copy-start | bytes 786436
  600.4 2.7 copy-start.10
  600.4 2.7 copy-start.11
  600.4 2.7 copy-start.12
  604.8 13.3 %copy-start.16 = (f32[32]{0:T(128)S(1)}, f32[32]{0:T(128)}, u32[]{:S(2)}) copy-start(f32[32]{0:T(128)} %get-tuple-element.49) | copy-start | bytes 388
  604.8 13.3 %copy-start.19 = (f32[32]{0:T(128)S(1)}, f32[32]{0:T(128)}, u32[]{:S(2)}) copy-start(f32[32]{0:T(128)} %get-tuple-element.131) | copy-start | bytes 388
  605.0 141.6 %copy-start.15 = (f32[128]{0:T(128)S(1)}, f32[128]{0:T(128)}, u32[]{:S(2)}) copy-start(f32[128]{0:T(128)} %param.17) | copy-start | bytes 1540
  611.9 136.5 %all-to-all-start.2 = ((f32[32,2,2,4,128]{4,1,3,2,0:T(2,128)}), f32[32,2,2,4,128]{4,1,3,2,0:T(2,128)S(1)}, u32[]{:S(2)}, u32[]{:S(2)}) async-start(f32[32,2,2,4,128]{4,1,3,2,0:T(2,128)} %copy.228), calls=%async_computation.2 | async-start | bytes 524288 | tf_op jit(solution)/shard_map/all_to_all | solution.py:47
  749.3 59.3 %copy-start.2 = (f32[1,2,256,256]{3,2,0,1:T(8,128)S(1)}, f32[1,2,256,256]{3,2,0,1:T(8,128)}, u32[]{:S(2)}) copy-start(f32[1,2,256,256]{3,2,0,1:T(8,128)} %get-tuple-element.87) | copy-start | bytes 1572868
  749.3 59.3 %copy-start.3 = (f32[1,2,256,256]{3,2,0,1:T(8,128)S(1)}, f32[1,2,256,256]{3,2,0,1:T(8,128)}, u32[]{:S(2)}) copy-start(f32[1,2,256,256]{3,2,0,1:T(8,128)} %get-tuple-element.90) | copy-start | bytes 1572868
  810.1 61.6 %copy-start.7 = (f32[1,1,64,4,256]{4,2,0,3,1:T(8,128)S(1)}, f32[1,1,64,4,256]{4,2,0,3,1:T(8,128)}, u32[]{:S(2)}) copy-start(f32[1,1,64,4,256]{4,2,0,3,1:T(8,128)} %copy-done.6) | copy-start | bytes 786436
  810.1 61.6 %copy-start.8 = (f32[1,1,64,4,256]{4,2,0,3,1:T(8,128)S(1)}, f32[1,1,64,4,256]{4,2,0,3,1:T(8,128)}, u32[]{:S(2)}) copy-start(f32[1,1,64,4,256]{4,2,0,3,1:T(8,128)} %get-tuple-element.122) | copy-start | bytes 786436
  810.1 61.7 %copy-start.9 = (f32[1,1,64,4,256]{4,2,0,3,1:T(8,128)S(1)}, f32[1,1,64,4,256]{4,2,0,3,1:T(8,128)}, u32[]{:S(2)}) copy-start(f32[1,1,64,4,256]{4,2,0,3,1:T(8,128)} %get-tuple-element.123) | copy-start | bytes 786436
  810.1 61.7 %copy-start.18 = (f32[4,256]{1,0:T(4,128)S(1)}, f32[4,256]{1,0:T(4,128)}, u32[]{:S(2)}) copy-start(f32[4,256]{1,0:T(4,128)} %param.16) | copy-start | bytes 12292
  810.1 61.4 %all-to-all-start.3 = ((f32[2,256,128]{2,0,1:T(2,128)}), f32[2,256,128]{2,0,1:T(2,128)S(1)}, u32[]{:S(2)}, u32[]{:S(2)}) async-start(f32[2,256,128]{2,0,1:T(2,128)} %copy.236), calls=%async_computation.3 | async-start | bytes 524288 | tf_op jit(solution)/shard_map/all_to_all | solution.py:142
Sparse Core Ops, SparseCore 0:
  10.8 72.2 all-gather.1
  89.2 228.1 all-reduce.9
  320.3 70.2 all-reduce.11
where the time goes:
time: 997 us; the launch traced here: 991 us
  waiting for transfers between devices  443 us (44%)
  blocking collectives  310 us (31%)
  other arithmetic  121 us (12%)
  starting transfers between devices  50.8 us (5%)
  matrix products  28.2 us (3%)
  local copies, waits for them, and re-layouts  19 us (2%)
  between operations  17.9 us (2%)
    psum x2, waiting for transfers between devices, by_axis(): return functools.reduce(lax.psum, axes, shard)  300 us
    psum x6, blocking collectives, by_axis(): return functools.reduce(lax.psum, axes, shard)  294 us
    all_to_all x2, waiting for transfers between devices, body(): lax.all_to_all(sectioned, PW, split_axis=1, concat_axis=2, tiled=True)  74.4 us
    another operation x14, other arithmetic, invert(): lower_factor = jnp.linalg.cholesky(normal)  69.2 us
    all_gather x1, waiting for transfers between devices, sent_together(): lax.all_gather(both, axis, axis=dim, tiled=True)  68.9 us
    all_to_all x2, starting transfers between devices, body(): lax.all_to_all(sectioned, PW, split_axis=1, concat_axis=2, tiled=True)  45.8 us
    another operation x5, other arithmetic, invert(): lax.linalg.triangular_solve(lower_factor, middle, left_side=True, lower=T...  39.6 us
  transfers between devices with their start and end apart: 6, of which 5 were waited for; matrix products, arithmetic and copies ran while one was open for 2% of the time, Pallas kernels for 0%

commit v1 on v0

v1 whole, which is shorter than its diff:
```python
import functools
import math

import jax
import jax.numpy as jnp
import ml_dtypes
import numpy as np
from jax import lax
from jax.experimental import pallas as pl
from jax.experimental.pallas import tpu as pltpu
from jax.sharding import PartitionSpec as P

MESH = pl.DeviceIdType.MESH
HIGHEST = lax.Precision.HIGHEST
string_step = 0.05
kinetic_scale = 4.0
LANES = 128
TILE = 8

NN = (((1,), (0,)), ((), ()))
NT = (((1,), (1,)), ((), ()))


def exact(a, b, dims=NN):
    return lax.dot_general(a, b, dims, precision=HIGHEST, preferred_element_type=jnp.float32)


def single(a, b, dims):
    return lax.dot_general(a, b, dims, preferred_element_type=jnp.float32)


def halves(a):
    high = a.astype(jnp.bfloat16)
    low = (a - high.astype(jnp.float32)).astype(jnp.bfloat16)
    return high, low


def triple(a, b, dims=NN):
    (ah, al), (bh, bl) = a, b
    return single(ah, bh, dims) + (single(ah, bl, dims) + single(al, bh, dims))


def iota(shape, dim):
    return lax.broadcasted_iota(jnp.int32, shape, dim)


def swap_blocks(tiles):
    u = iota(tiles.shape, 1) % 4
    w = iota(tiles.shape, 2) // (LANES // 4)
    turned = pltpu.roll(tiles, LANES // 2, 2)
    below, above = pltpu.roll(turned, TILE - 2, 1), pltpu.roll(turned, 2, 1)
    same, upper = (u // 2) == (w // 2), (u // 2) < (w // 2)
    tiles = jnp.where(same, tiles, jnp.where(upper, below, above))
    below = pltpu.roll(pltpu.roll(tiles, LANES // 4, 2), TILE - 1, 1)
    above = pltpu.roll(pltpu.roll(tiles, LANES - LANES // 4, 2), 1, 1)
    same, upper = (u % 2) == (w % 2), (u % 2) < (w % 2)
    return jnp.where(same, tiles, jnp.where(upper, below, above))


def kernel(
    n, nx, points,
    w_ref, f_ref, b_ref, p_ref, diag_ref, pot_ref, str_ref,
    t2h_ref, t2l_ref, t1h_ref, t1l_ref, t3h_ref, t3l_ref,
    der_ref, sol_ref,
    ph_ref, pl_ref, near, mpart, mrs, mfull, mall, nmat, zmat,
    vec, res, img,
    sendb, recvb, sendc, recvc, sende, recve,
    cpart, crs, cfull, cpart2, crs2,
    scal, scals, scal2, scals2, field_ref,
    xs, xr, ms, mr, cs, cr, es, er,
):
    me = lax.axis_index("pw")
    mx = lax.axis_index("band")
    bands = w_ref.shape[0] // 4
    half = w_ref.shape[1] // 2
    every = nx * bands
    right, left = lax.rem(mx + 1, nx), lax.rem(mx + nx - 1, nx)

    def other(i):
        part = (i + 1) // 2
        return lax.rem(me + n // 2 + part * (2 * lax.rem(i, 2) - 1) + n, n)

    barrier = pltpu.get_barrier_semaphore()

    def greet(i, carry):
        pl.semaphore_signal(barrier, inc=1, device_id={"pw": other(i)}, device_id_type=MESH)
        return carry

    lax.fori_loop(0, n - 1, greet, 0)
    for step in range(1, nx):
        pl.semaphore_signal(
            barrier, inc=1, device_id={"band": lax.rem(mx + step, nx)}, device_id_type=MESH
        )
    pl.semaphore_wait(barrier, n - 1 + nx - 1)

    def remote(src, dst, send, recv, axis, target):
        return pltpu.make_async_remote_copy(
            src_ref=src, dst_ref=dst, send_sem=send, recv_sem=recv,
            device_id={axis: target}, device_id_type=MESH,
        )

    def exchange(src, dst, send, recv):
        dst[pl.ds(me, 1)] = src[pl.ds(me, 1)]

        def one(i, carry):
            t = other(i)
            remote(src.at[t], dst.at[me], send, recv, "pw", t).start()
            return carry

        lax.fori_loop(0, n - 1, one, 0)

    def tell(src, dst, send, recv):
        def one(i, carry):
            remote(src, dst, send, recv, "pw", other(i)).start()
            return carry

        lax.fori_loop(0, n - 1, one, 0)

    def arrived(dst, count, recv):
        some = dst.at[pl.ds(0, count)]
        remote(some, some, recv, recv, "pw", other(0)).wait_recv()

    def left_here(src, count, send):
        some = src.at[pl.ds(0, count)]
        remote(some, some, send, send, "pw", other(0)).wait_send()

    def to_owners(src, dst, send, recv):
        tiles = src.shape[0]
        stride = n // tiles

        def one(i, carry):
            t = lax.rem(i + me // stride, tiles)
            owner = t * stride

            @pl.when(owner != me)
            def _():
                remote(src.at[t], dst.at[me], send, recv, "pw", owner).start()

            @pl.when(owner == me)
            def _():
                dst[pl.ds(me, 1)] = src[pl.ds(t, 1)]

            return carry

        lax.fori_loop(0, tiles, one, 0)

    def sent_to_owners(src, send):
        tiles = src.shape[0]
        owns = lax.rem(me, n // tiles) == 0

        @pl.when(owns)
        def _():
            left_here(src, tiles - 1, send)

        @pl.when(jnp.logical_not(owns))
        def _():
            left_here(src, tiles, send)

    def owners_tell(buf, full, recv, tell_send, tell_recv):
        tiles = full.shape[0]
        stride = n // tiles

        @pl.when(lax.rem(me, stride) == 0)
        def _():
            arrived(buf, n - 1, recv)
            t = me // stride
            full[pl.ds(t, 1)] = jnp.sum(buf[...], axis=0, keepdims=True)
            tell(full.at[t], full.at[t], tell_send, tell_recv)

    def told(full, recv):
        tiles = full.shape[0]
        owns = lax.rem(me, n // tiles) == 0

        @pl.when(owns)
        def _():
            arrived(full, tiles - 1, recv)

        @pl.when(jnp.logical_not(owns))
        def _():
            arrived(full, tiles, recv)

    def owners_done(buf, full, send):
        tiles = full.shape[0]

        @pl.when(lax.rem(me, n // tiles) == 0)
        def _():
            left_here(buf, n - 1, send)

    near[0, 0] = f_ref[...]
    near[0, 1] = b_ref[...]
    to_right = [
        remote(f_ref, near.at[3, 0], xs.at[0], xr.at[0], "band", right),
        remote(b_ref, near.at[3, 1], xs.at[1], xr.at[1], "band", right),
    ]
    to_left = [
        remote(b_ref, near.at[1, 1], xs.at[2], xr.at[2], "band", left),
        remote(f_ref, near.at[1, 0], xs.at[3], xr.at[3], "band", left),
    ]
    for a, b in zip(to_right, to_left):
        a.start()
        b.start()

    ph_ref[...], pl_ref[...] = halves(p_ref[...])
    own = []
    for r in range(4):
        rows = w_ref[r * bands : (r + 1) * bands, :]
        own.append(jnp.concatenate([rows, jnp.concatenate([-rows[:, half:], rows[:, :half]], 1)], 0))

    def margin_of(slot, which):
        total = None
        for r in range(4):
            term = exact(own[r], near[slot, which, r * bands : (r + 1) * bands, :], NT)
            total = term if total is None else total + term
        mpart_rows = pl.ds(which * 2 * bands, 2 * bands)
        nmat[0, 0, mpart_rows, slot * bands : (slot + 1) * bands] = total

    margin_of(0, 0)
    margin_of(0, 1)
    to_right[0].wait_recv()
    far_right = remote(near.at[3, 0], near.at[2, 0], xs.at[4], xr.at[4], "band", right)
    far_right.start()
    to_left[0].wait_recv()
    far_left = remote(near.at[1, 1], near.at[2, 1], xs.at[5], xr.at[5], "band", left)
    far_left.start()
    margin_of(3, 0)
    margin_of(1, 1)
    to_right[1].wait_recv()
    to_left[1].wait_recv()
    margin_of(3, 1)
    margin_of(1, 0)
    far_right.wait_recv()
    margin_of(2, 0)
    far_left.wait_recv()
    margin_of(2, 1)
    turned = pltpu.roll(nmat[0, 0], mx * bands, 1)
    mpart[...] = turned.reshape(mpart.shape)

    to_owners(mpart, mrs, ms.at[0], mr.at[0])
    owners_tell(mrs, mfull, mr.at[0], ms.at[1], mr.at[1])
    told(mfull, mr.at[1])
    mall[pl.ds(mx, 1)] = mfull[...][None]
    for step in range(1, nx):
        t = lax.rem(mx + step, nx)
        remote(mfull, mall.at[mx], ms.at[2], mr.at[2], "band", t).start()
    some = mall.at[pl.ds(0, nx - 1)]
    across = remote(some, some, ms.at[2], mr.at[2], "band", right)
    across.wait_recv()

    def margin_full(which, part):
        tiles_each = bands // TILE
        at = (which * 2 + part) * tiles_each
        rows = [mall[x, at : at + tiles_each].reshape(bands, every) for x in range(nx)]
        return jnp.concatenate(rows, 0) / points

    for which in range(2):
        real, imag = margin_full(which, 0), margin_full(which, 1)
        nmat[which, 0] = exact(real, real, NT) + exact(imag, imag, NT)
        nmat[which, 1] = exact(real, imag, NT) - exact(imag, real, NT)

    def eliminate(c, carry):
        lane = iota((every, every), 1)
        row = iota((every, every), 0)
        on_lane, on_row = lane == c, row == c
        at = jnp.full((every, every), 0, jnp.int32) + c
        for which in range(2):
            real, imag = nmat[which, 0], nmat[which, 1]
            row_r = nmat[which, 0, pl.ds(c, 1), :]
            row_i = nmat[which, 1, pl.ds(c, 1), :]
            col_r = jnp.take_along_axis(real, at, axis=1)
            col_i = jnp.take_along_axis(imag, at, axis=1)
            pivot = jnp.sum(jnp.where(lane[:1] == c, row_r, 0.0), axis=1, keepdims=True)
            scale = 1.0 / pivot
            row_r = jnp.where(lane[:1] == c, 1.0, row_r) * scale
            row_i = jnp.where(lane[:1] == c, 0.0, row_i) * scale
            real = jnp.where(on_lane, 0.0, real) - (col_r * row_r - col_i * row_i)
            imag = jnp.where(on_lane, 0.0, imag) - (col_r * row_i + col_i * row_r)
            nmat[which, 0] = jnp.where(on_row, row_r, real)
            nmat[which, 1] = jnp.where(on_row, row_i, imag)
        return carry

    lax.fori_loop(0, every, eliminate, 0)

    for which in range(2):
        real, imag = margin_full(which, 0), margin_full(which, 1)
        mine = pl.ds(pl.multiple_of(mx * bands, TILE), bands)
        nr, ni = nmat[which, 0, mine, :], nmat[which, 1, mine, :]
        zr = exact(nr, real) + exact(ni, imag)
        zi = exact(ni, real) - exact(nr, imag)
        both = pltpu.roll(jnp.concatenate([zr, zi], 0), lax.rem((nx - mx) * bands, every), 1)
        zmat[:, which * every : (which + 1) * every] = both if which == 0 else -both

    coeff = zmat[...]
    for r in range(4):
        rows = slice(r * bands, (r + 1) * bands)
        blocks = [near[d, which, rows, :] for which in range(2) for d in range(nx)]
        mixed = exact(coeff, jnp.concatenate(blocks, 0))
        dr = (mixed[:bands, :half] - mixed[bands:, half:]) / (2.0 * string_step)
        di = (mixed[:bands, half:] + mixed[bands:, :half]) / (2.0 * string_step)
        der_ref[rows, :half] = dr
        der_ref[rows, half:] = di
        vec[rows, :half] = -dr
        vec[rows, half:] = -di

    def forth(src, send, recv, sem):
        parts = halves(src[...])
        out = triple((t2h_ref[...], t2l_ref[...]), parts, NT)
        send[...] = swap_blocks(out.reshape(n, TILE, LANES))
        exchange(send, recv, es.at[sem], er.at[sem])

    def fields(recv, sem):
        arrived(recv, n - 1, er.at[sem])
        parts = halves(recv[...].reshape(n * TILE, LANES))
        return triple((t1h_ref[...], t1l_ref[...]), parts)

    def project(src, part, buf, send, recv):
        total = None
        for r in range(4):
            rows = src[r * bands : (r + 1) * bands, :]
            both = jnp.concatenate([rows, jnp.concatenate([rows[:, half:], -rows[:, :half]], 1)], 0)
            at = slice(r * every, (r + 1) * every)
            term = triple(halves(both), (ph_ref[at, :], pl_ref[at, :]), NT)
            total = term if total is None else total + term
        part[...] = (total / points).reshape(part.shape)
        to_owners(part, buf, send, recv)

    def per_band(values):
        return sum(values[r * bands : (r + 1) * bands] for r in range(1, 4)) + values[:bands]

    def summed(values):
        return per_band(jnp.sum(values, axis=1, keepdims=True))

    def as_row(column, first):
        shape = (column.shape[0], LANES)
        chosen = iota(shape, 1) == iota(shape, 0) + first
        return jnp.sum(jnp.where(chosen, column, 0.0), axis=0, keepdims=True)

    def as_column(row, first):
        shape = (bands, LANES)
        chosen = iota(shape, 1) == iota(shape, 0) + first
        return jnp.sum(jnp.where(chosen, row, 0.0), axis=1, keepdims=True)

    def lanes_per_band(row, first):
        row = row + pltpu.roll(row, LANES // 2, 1)
        row = row + pltpu.roll(row, LANES // 4, 1)
        lane = iota(row.shape, 1)
        return jnp.where((lane >= first) & (lane < first + bands), row, 0.0)

    def down_rows(column):
        return jnp.concatenate([column] * 4, 0)

    diag = jnp.concatenate([diag_ref[...]] * 2, 1)
    stren = str_ref[...]

    forth(vec, sendb, recvb, 0)
    project(vec, cpart, crs, cs.at[0], cr.at[0])
    d = vec[...]
    scal_row = as_row(summed(diag * d * d), 0) + as_row(summed(d * d), 2 * bands)
    owners_tell(crs, cfull, cr.at[0], cs.at[1], cr.at[1])
    field = fields(recvb, 0)
    field_ref[...] = field
    pot = jnp.concatenate([pot_ref[...]] * 2, 0)
    weighted = field * pot
    energy = jnp.sum(weighted * field, axis=0, keepdims=True)
    sendc[...] = triple((t3h_ref[...], t3l_ref[...]), halves(weighted)).reshape(sendc.shape)
    scal[...] = scal_row + lanes_per_band(energy, 0)
    tell(scal, scals.at[me], es.at[3], er.at[3])
    exchange(sendc, recvc, es.at[1], er.at[1])
    scals[pl.ds(me, 1)] = scal[...][None]

    told(cfull, cr.at[1])
    coupled = cfull[...].reshape(2 * bands, every)
    weights = halves(coupled * stren)
    for r in range(4):
        at = slice(r * every, (r + 1) * every)
        rows = slice(r * bands, (r + 1) * bands)
        mixed = triple(weights, (ph_ref[at, :], pl_ref[at, :]))
        img[rows, :half] = mixed[:bands, :half] - mixed[bands:, half:]
        img[rows, half:] = mixed[:bands, half:] + mixed[bands:, :half]
    pair = jnp.sum(stren * coupled * coupled, axis=1, keepdims=True)
    own_pair = points * (pair[:bands] + pair[bands:])
    arrived(scals, n - 1, er.at[3])
    totals = jnp.sum(scals[...], axis=0)
    norm_now = as_column(totals, 2 * bands)
    curvature = as_column(totals, 0) + own_pair
    alpha = norm_now / curvature

    arrived(recvc, n - 1, er.at[1])
    back = swap_blocks(recvc[...]).reshape(n * TILE, LANES).T
    smooth = triple(halves(back), (t2h_ref[...], t2l_ref[...]))
    d = vec[...]
    image = diag * d + smooth + img[...]
    res[...] = d - down_rows(alpha) * image

    forth(res, sende, recve, 2)
    project(res, cpart2, crs2, cs.at[2], cr.at[2])
    d, r2 = vec[...], res[...]
    stiff = diag * r2
    row2 = as_row(summed(stiff * r2), 0) + as_row(summed(stiff * d), bands)
    row2 = row2 + as_row(summed(r2 * r2), 2 * bands)
    scal2[...] = row2
    tiles2 = cpart2.shape[0]
    stride2 = n // tiles2

    @pl.when(lax.rem(me, stride2) == 0)
    def _():
        arrived(crs2, n - 1, cr.at[2])
        t = me // stride2
        mine = jnp.sum(crs2[...], axis=0)
        old = cfull[pl.ds(t, 1)].reshape(TILE, every)
        first = lax.rem(t * TILE, bands)
        with_mine = points * jnp.sum(stren * mine * mine, axis=1, keepdims=True)
        with_old = points * jnp.sum(stren * mine * old, axis=1, keepdims=True)
        scal2[...] = scal2[...] + as_row(with_mine, first) + as_row(with_old, first + bands)

    field2 = fields(recve, 2)
    weighted2 = field2 * jnp.concatenate([pot_ref[...]] * 2, 0)
    own2 = jnp.sum(weighted2 * field2, axis=0, keepdims=True)
    cross2 = jnp.sum(weighted2 * field_ref[...], axis=0, keepdims=True)
    scal2[...] = scal2[...] + lanes_per_band(own2, 0) + lanes_per_band(cross2, bands)
    tell(scal2, scals2.at[me], es.at[4], er.at[4])
    scals2[pl.ds(me, 1)] = scal2[...][None]
    arrived(scals2, n - 1, er.at[4])
    totals2 = jnp.sum(scals2[...], axis=0)
    norm_next = as_column(totals2, 2 * bands)
    beta = norm_next / norm_now
    curvature2 = (
        as_column(totals2, 0) + 2.0 * beta * as_column(totals2, bands) + beta * beta * curvature
    )
    alpha2 = norm_next / curvature2
    sol_ref[...] = down_rows(alpha + alpha2 * beta) * vec[...] + down_rows(alpha2) * res[...]

    for copy in to_right + to_left + [far_right, far_left]:
        copy.wait_send()
    across.wait_send()
    sent_to_owners(mpart, ms.at[0])
    owners_done(mrs, mfull, ms.at[1])
    sent_to_owners(cpart, cs.at[0])
    owners_done(crs, cfull, cs.at[1])
    sent_to_owners(cpart2, cs.at[2])
    left_here(sendb, n - 1, es.at[0])
    left_here(sendc, n - 1, es.at[1])
    left_here(sende, n - 1, es.at[2])
    left_here(scals, n - 1, es.at[3])
    left_here(scals2, n - 1, es.at[4])


def centred(index, length):
    shifted = (index + length // 2) % length - length // 2
    return shifted.astype(jnp.float32) / length


def split_table(table):
    table = table.astype(np.float32)
    high = table.astype(ml_dtypes.bfloat16)
    low = (table - high.astype(np.float32)).astype(ml_dtypes.bfloat16)
    return high, low


def tables(length, peers):
    index = np.arange(length)
    angle = (index[:, None] * index[None, :] % length) * (2.0 * math.pi / length)
    cosine, sine = np.cos(angle) / math.sqrt(length), np.sin(angle) / math.sqrt(length)
    out = np.block([[cosine, -sine], [sine, cosine]])
    order = np.arange(2 * length).reshape(2, peers, length // peers).transpose(1, 0, 2).reshape(-1)
    first, third = out[order], out.T[order]
    return (*split_table(first), *split_table(third.T.copy()), *split_table(third))


def flat(array):
    items, parts, rows, width = array.shape
    return array.transpose(2, 0, 1, 3).reshape(rows * items, parts * width)


def body(n, nx, waves, forward, backward, projectors, potential, strengths, shifts):
    bands, parts, rows, width = waves.shape
    length = rows * n
    points = float(length * width)
    every = nx * bands
    count = projectors.shape[0]
    first_index = lax.axis_index("pw") * rows + jnp.arange(rows, dtype=jnp.int32)
    second_index = jnp.arange(width, dtype=jnp.int32)
    first_freq, second_freq = centred(first_index, length), centred(second_index, width)
    kinetic = kinetic_scale * (
        first_freq[:, None] * first_freq[:, None] + second_freq[None, :] * second_freq[None, :]
    )
    diag = (kinetic[:, None, :] + shifts[None, :, None]).reshape(rows * bands, width)
    pot = jnp.repeat(potential.T, bands, axis=1)
    shape = (rows * bands, parts * width)
    f32 = functools.partial(pltpu.VMEM, dtype=jnp.float32)
    full, tiles = (n, TILE, LANES), 2 * bands // TILE
    vmem = pl.BlockSpec(memory_space=pltpu.VMEM)
    dma = pltpu.SemaphoreType.DMA
    der, sol = pl.pallas_call(
        functools.partial(kernel, n, nx, points),
        out_shape=[jax.ShapeDtypeStruct(shape, jnp.float32)] * 2,
        in_specs=[vmem] * 13,
        out_specs=[vmem] * 2,
        scratch_shapes=[
            pltpu.VMEM((rows * count, parts * width), jnp.bfloat16),
            pltpu.VMEM((rows * count, parts * width), jnp.bfloat16),
            f32((nx, 2, *shape)),
            f32((2 * tiles, TILE, LANES)), f32(full), f32((2 * tiles, TILE, LANES)),
            f32((nx, 2 * tiles, TILE, LANES)), f32((2, 2, every, every)), f32((2 * bands, 2 * every)),
            f32(shape), f32(shape), f32(shape),
            f32(full), f32(full), f32(full), f32(full), f32(full), f32(full),
            f32((tiles, TILE, LANES)), f32(full), f32((tiles, TILE, LANES)),
            f32((tiles, TILE, LANES)), f32(full),
            f32((1, LANES)), f32((n, 1, LANES)), f32((1, LANES)), f32((n, 1, LANES)),
            f32((n * TILE, LANES)),
            dma((6,)), dma((6,)), dma((3,)), dma((3,)), dma((3,)), dma((3,)), dma((5,)), dma((5,)),
        ],
        compiler_params=pltpu.CompilerParams(
            collective_id=0, has_side_effects=True, vmem_limit_bytes=60 * 1024 * 1024
        ),
    )(
        flat(waves), flat(forward), flat(backward), flat(projectors), diag, pot,
        strengths.reshape(1, count), *[jnp.asarray(t) for t in tables(length, n)],
    )

    def unflat(array):
        return array.reshape(rows, bands, parts, width).transpose(1, 2, 0, 3)

    return unflat(sol), unflat(der)


def solution(mesh):
    bands = P("band", "kgrp", "pw", None)
    return jax.shard_map(
        functools.partial(body, mesh.shape["pw"], mesh.shape["band"]),
        mesh=mesh,
        in_specs=(bands, bands, bands, P("kgrp", None, "pw", None), P("pw", None), P(), P("band")),
        out_specs=(bands, bands),
        check_vma=False,
    )
```

time: 997 us -> 279 us (0.28)
  waiting for transfers between devices: 443 us -> 0 us
  blocking collectives: 310 us -> 0 us
  Pallas kernels: 0 us -> 267 us
  other arithmetic: 121 us -> 0.84 us
  starting transfers between devices: 50.8 us -> 0 us
  matrix products: 28.2 us -> 0 us
  between operations: 17.9 us -> 0.73 us
    psum x2 -> x0, waiting for transfers between devices: 300 us -> none  [by_axis(): return functools.reduce(lax.psum, axes, shard)]
    psum x6 -> x0, blocking collectives: 294 us -> none  [by_axis(): return functools.reduce(lax.psum, axes, shard)]
    pallas_call x0 -> x1, Pallas kernels: none -> 267 us  [body(): pl.pallas_call(functools.partial(kernel, n, nx, points), out_shape=[jax.S...]
    another operation x23 -> x0, other arithmetic: 110 us -> none  [the longest x14 69.2 us: invert(): lower_factor = jnp.linalg.cholesky(normal)]
    all_to_all x3 -> x0, waiting for transfers between devices: 74.4 us -> none  [the longest x2 74.4 us: body(): lax.all_to_all(sectioned, PW, split_axis=1, concat_axis=2, tiled=True)]
    all_gather x1 -> x0, waiting for transfers between devices: 68.9 us -> none  [sent_together(): lax.all_gather(both, axis, axis=dim, tiled=True)]
    all_to_all x3 -> x0, starting transfers between devices: 50.6 us -> none  [the longest x2 45.8 us: body(): lax.all_to_all(sectioned, PW, split_axis=1, concat_axis=2, tiled=True)]
    dot_general x15 -> x0, matrix products: 22 us -> none  [the longest x4 6.94 us: margin(): jnp.einsum('ixg,jyg->xyij', left_set, right_set, precision=precise)]
  transfers between devices with their start and end apart: 6 -> 0, of which waited for: 5 -> 0; matrix products, arithmetic and copies ran while one was open for 2% -> 0% of each run, Pallas kernels for 0% -> 0%
where the time goes in v1:
time: 279 us
  Pallas kernels  267 us (96%)
  local copies, waits for them, and re-layouts  9.9 us (4%)
    pallas_call x1, Pallas kernels, body(): pl.pallas_call(functools.partial(kernel, n, nx, points), out_shape=[jax.S...  267 us

profile of v1, /device:TPU:33, one launch (start us, length us, event | category | flops | bytes accessed | tf_op | source)
XLA Modules:
  0.0 278.8 jit_solution(13833652656774980424)
XLA Ops:
  0.6 1.8 copy.25
  2.4 0.0 copy-start
  2.4 1.0 copy.32
  3.4 0.0 copy-done
  3.4 0.1 copy.22
  3.6 0.0 copy-start.1
  3.6 0.7 copy.29
  4.3 0.3 copy-done.1
  4.6 0.1 copy.23
  4.8 0.0 copy-start.2
  4.8 0.7 copy.30
  5.5 0.3 copy-done.2
  5.8 0.1 copy.24
  6.0 0.0 copy-start.4
  6.0 0.7 copy.31
  6.7 0.0 copy-done.4
  6.7 0.8 copy.26.pot_ref
  7.5 0.0 copy-start.5
  7.5 0.1 add_multiply_fusion
  7.6 0.6 copy-done.5
  8.1 0.1 add.103
  8.2 0.7 bitcast_add_fusion.diag_ref
  9.0 267.3 %shard_map.140 = (f32[128,512]{1,0:T(8,128)}, f32[128,512]{1,0:T(8,128)}) custom-call(f32[128,512]{1,0:T(8,128)} %bitcast.31, f32[128,512]{1,0:T(8,128)} %bitcast.32, f32[128,512]{1,0:T(8,128)} %bitcast.33, f32[512,512]{1,0:T(8,128)} %bitcast.26, f32[128,256]{1,0:T(8,128)} %bitcast_add_fusion.diag_ref, f32[256,128]{1,0:T(8,128)} %copy.26.pot_ref, ...), custom_call_target="tpu_custom_call" | custom-call | tf_op jit(solution)/shard_map/pallas_call | solution.py:493
  276.3 0.0 copy-start.3
  276.3 1.2 reshape.103
  277.5 0.0 copy-done.3
  277.5 0.2 reshape.104
  277.7 1.1 copy_bitcast_fusion
  (4 shorter events, 0.0 us)
Async XLA Ops:
  2.4 1.1 copy-start
  3.6 1.0 copy-start.1
  4.8 1.0 copy-start.2
  6.0 0.7 copy-start.4
  7.5 0.7 copy-start.5
  276.3 1.2 copy-start.3

commit v2 on v1

--- a/solution.py
+++ b/solution.py
@@ -59,15 +59,16 @@
 
 def kernel(
     n, nx, points,
-    w_ref, f_ref, b_ref, p_ref, diag_ref, pot_ref, str_ref,
-    t2h_ref, t2l_ref, t1h_ref, t1l_ref, t3h_ref, t3l_ref,
-    der_ref, sol_ref,
-    ph_ref, pl_ref, near, mpart, mrs, mfull, mall, nmat, zmat,
+    w_raw, f_raw, b_raw, p_ref, shift_ref, pot_ref, str_ref,
+    t2h_ref, t2l_ref,
+    der_raw, sol_raw,
+    w_ref, f_ref, b_ref,
+    diag_ref, pots_ref, ph_ref, pl_ref, t1h_ref, t1l_ref, t3h_ref, t3l_ref, wide, qt, near, mpart, mrs, mfull, mall, nmat, zmat,
     vec, res, img,
     sendb, recvb, sendc, recvc, sende, recve,
     cpart, crs, cfull, cpart2, crs2,
     scal, scals, scal2, scals2, field_ref,
-    xs, xr, ms, mr, cs, cr, es, er,
+    known, xs, xr, ms, mr, cs, cr, es, er,
 ):
     me = lax.axis_index("pw")
     mx = lax.axis_index("band")
@@ -80,18 +81,44 @@
         part = (i + 1) // 2
         return lax.rem(me + n // 2 + part * (2 * lax.rem(i, 2) - 1) + n, n)
 
+
+    def flatten(raw, flat_ref):
+        for r in range(4):
+            for part in range(2):
+                lanes = slice(part * half, (part + 1) * half)
+                flat_ref[r * bands : (r + 1) * bands, lanes] = raw[:, part, r, :]
+
     barrier = pltpu.get_barrier_semaphore()
 
-    def greet(i, carry):
-        pl.semaphore_signal(barrier, inc=1, device_id={"pw": other(i)}, device_id_type=MESH)
-        return carry
-
-    lax.fori_loop(0, n - 1, greet, 0)
+    def at_distance(d):
+        return lax.rem(me + d + n, n)
+
+    def greet(d, axis="pw", base=None):
+        target = at_distance(d) if base is None else base
+        pl.semaphore_signal(barrier, inc=1, device_id={axis: target}, device_id_type=MESH)
+
+    partner = me + 1 - 2 * lax.rem(me, 2)
+    greet(0, "pw", partner)
+    greet(2)
+    greet(-2)
     for step in range(1, nx):
-        pl.semaphore_signal(
-            barrier, inc=1, device_id={"band": lax.rem(mx + step, nx)}, device_id_type=MESH
-        )
-    pl.semaphore_wait(barrier, n - 1 + nx - 1)
+        greet(0, "band", lax.rem(mx + step, nx))
+    flatten(w_raw, w_ref)
+    flatten(f_raw, f_ref)
+    flatten(b_raw, b_ref)
+    pl.semaphore_wait(barrier, 3 + nx - 1)
+
+    def learn(k):
+        d = 2 << k
+        for target in (at_distance(d), at_distance(-d)):
+            pl.semaphore_signal(known.at[k], inc=1, device_id={"pw": target}, device_id_type=MESH)
+        pl.semaphore_wait(known.at[k], 2)
+
+    rounds = (n // 4).bit_length() - 1
+
+    def learn_partner():
+        pl.semaphore_signal(known.at[rounds], inc=1, device_id={"pw": partner}, device_id_type=MESH)
+        pl.semaphore_wait(known.at[rounds], 1)
 
     def remote(src, dst, send, recv, axis, target):
         return pltpu.make_async_remote_copy(
@@ -99,22 +126,22 @@
             device_id={axis: target}, device_id_type=MESH,
         )
 
+    group = max(k for k in (1, 3, 7, 9) if (n - 1) % k == 0)
+
+    def to_others(start):
+        def some(i, carry):
+            for k in range(group):
+                start(other(i * group + k))
+            return carry
+
+        lax.fori_loop(0, (n - 1) // group, some, 0)
+
     def exchange(src, dst, send, recv):
         dst[pl.ds(me, 1)] = src[pl.ds(me, 1)]
-
-        def one(i, carry):
-            t = other(i)
-            remote(src.at[t], dst.at[me], send, recv, "pw", t).start()
-            return carry
-
-        lax.fori_loop(0, n - 1, one, 0)
+        to_others(lambda t: remote(src.at[t], dst.at[me], send, recv, "pw", t).start())
 
     def tell(src, dst, send, recv):
-        def one(i, carry):
-            remote(src, dst, send, recv, "pw", other(i)).start()
-            return carry
-
-        lax.fori_loop(0, n - 1, one, 0)
+        to_others(lambda t: remote(src, dst, send, recv, "pw", t).start())
 
     def arrived(dst, count, recv):
         some = dst.at[pl.ds(0, count)]
@@ -186,57 +213,98 @@
         def _():
             left_here(buf, n - 1, send)
 
-    near[0, 0] = f_ref[...]
-    near[0, 1] = b_ref[...]
+    part_rows = w_ref.shape[0] // 2
+    lower, upper = pl.ds(0, part_rows), pl.ds(part_rows, part_rows)
+
+    def over_band(src, dst, at, target):
+        return remote(src, dst, xs.at[at], xr.at[at], "band", target)
+
     to_right = [
-        remote(f_ref, near.at[3, 0], xs.at[0], xr.at[0], "band", right),
-        remote(b_ref, near.at[3, 1], xs.at[1], xr.at[1], "band", right),
+        over_band(w_ref.at[lower], wide.at[3, lower], 0, right),
+        over_band(w_ref.at[upper], wide.at[3, upper], 1, right),
+        over_band(f_ref, near.at[3, 0], 6, right),
+        over_band(b_ref, near.at[3, 1], 8, right),
     ]
     to_left = [
-        remote(b_ref, near.at[1, 1], xs.at[2], xr.at[2], "band", left),
-        remote(f_ref, near.at[1, 0], xs.at[3], xr.at[3], "band", left),
+        over_band(w_ref.at[upper], wide.at[1, upper], 2, left),
+        over_band(w_ref.at[lower], wide.at[1, lower], 3, left),
+        over_band(b_ref, near.at[1, 1], 9, left),
+        over_band(f_ref, near.at[1, 0], 7, left),
     ]
     for a, b in zip(to_right, to_left):
         a.start()
         b.start()
-
-    ph_ref[...], pl_ref[...] = halves(p_ref[...])
+    wide[0] = w_ref[...]
+    near[0, 0] = f_ref[...]
+    near[0, 1] = b_ref[...]
+    learn(0)
+    learn(1)
+
     own = []
     for r in range(4):
-        rows = w_ref[r * bands : (r + 1) * bands, :]
-        own.append(jnp.concatenate([rows, jnp.concatenate([-rows[:, half:], rows[:, :half]], 1)], 0))
-
-    def margin_of(slot, which):
+        both = []
+        for src in (f_ref, b_ref):
+            rows = src[r * bands : (r + 1) * bands, :]
+            both += [rows, jnp.concatenate([rows[:, half:], -rows[:, :half]], 1)]
+        own.append(halves(jnp.concatenate(both, 0)))
+
+    def margin_of(slot):
         total = None
         for r in range(4):
-            term = exact(own[r], near[slot, which, r * bands : (r + 1) * bands, :], NT)
+            term = triple(own[r], halves(wide[slot, r * bands : (r + 1) * bands, :]), NT)
             total = term if total is None else total + term
-        mpart_rows = pl.ds(which * 2 * bands, 2 * bands)
-        nmat[0, 0, mpart_rows, slot * bands : (slot + 1) * bands] = total
-
-    margin_of(0, 0)
-    margin_of(0, 1)
+        nmat[0, 0, :, slot * bands : (slot + 1) * bands] = total
+
     to_right[0].wait_recv()
-    far_right = remote(near.at[3, 0], near.at[2, 0], xs.at[4], xr.at[4], "band", right)
+    far_right = over_band(wide.at[3, lower], wide.at[2, lower], 4, right)
     far_right.start()
     to_left[0].wait_recv()
-    far_left = remote(near.at[1, 1], near.at[2, 1], xs.at[5], xr.at[5], "band", left)
+    far_left = over_band(wide.at[1, upper], wide.at[2, upper], 5, left)
     far_left.start()
-    margin_of(3, 0)
-    margin_of(1, 1)
+    learn(2)
+    margin_of(0)
     to_right[1].wait_recv()
+    margin_of(3)
     to_left[1].wait_recv()
-    margin_of(3, 1)
-    margin_of(1, 0)
+    margin_of(1)
+    for k in range(3, rounds):
+        learn(k)
+    learn_partner()
     far_right.wait_recv()
-    margin_of(2, 0)
     far_left.wait_recv()
-    margin_of(2, 1)
+    margin_of(2)
     turned = pltpu.roll(nmat[0, 0], mx * bands, 1)
     mpart[...] = turned.reshape(mpart.shape)
 
     to_owners(mpart, mrs, ms.at[0], mr.at[0])
+    for r in range(4):
+        for part in range(2):
+            rows = slice(r * every, (r + 1) * every)
+            lanes = slice(part * half, (part + 1) * half)
+            ph_ref[rows, lanes], pl_ref[rows, lanes] = halves(p_ref[:, part, r, :])
+    u = me * 4 + iota((4 * bands, half), 0) // bands
+    w = iota((4 * bands, half), 1)
+    u, w = centred(u, 4 * n), centred(w, half)
+    diag_ref[...] = kinetic_scale * (u * u + w * w) + shift_ref[...]
+    columns = jnp.concatenate([pot_ref[...]] * 2, 0).T
+    at = iota((4 * n, LANES), 1) // bands
+    spread = jnp.zeros((4 * n, LANES), jnp.float32)
+    for k in range(4):
+        spread = jnp.where(at == k, columns[:, k : k + 1], spread)
+    pots_ref[...] = spread
+    shape = t2h_ref.shape
+    row_part, lane_part = iota(shape, 0) % TILE // (TILE // 2), iota(shape, 1) // half
+    flip = jnp.where(row_part == lane_part, 1.0, -1.0)
+    inverse_table = (t2h_ref[...].astype(jnp.float32) + t2l_ref[...].astype(jnp.float32)) * flip
+    t3h_ref[...], t3l_ref[...] = halves(inverse_table)
+    t1h_ref[...], t1l_ref[...] = halves(inverse_table.T)
     owners_tell(mrs, mfull, mr.at[0], ms.at[1], mr.at[1])
+    to_right[2].wait_recv()
+    far_f = over_band(near.at[3, 0], near.at[2, 0], 10, right)
+    far_f.start()
+    to_left[2].wait_recv()
+    far_b = over_band(near.at[1, 1], near.at[2, 1], 11, left)
+    far_b.start()
     told(mfull, mr.at[1])
     mall[pl.ds(mx, 1)] = mfull[...][None]
     for step in range(1, nx):
@@ -255,40 +323,67 @@
     for which in range(2):
         real, imag = margin_full(which, 0), margin_full(which, 1)
         nmat[which, 0] = exact(real, real, NT) + exact(imag, imag, NT)
-        nmat[which, 1] = exact(real, imag, NT) - exact(imag, real, NT)
-
-    def eliminate(c, carry):
+        nmat[which, 1] = exact(imag, real, NT) - exact(real, imag, NT)
+        qt[which, 0] = real.T
+        qt[which, 1] = imag.T
+
+    def eliminate(step, carry):
+        c = 2 * step
         lane = iota((every, every), 1)
-        row = iota((every, every), 0)
-        on_lane, on_row = lane == c, row == c
-        at = jnp.full((every, every), 0, jnp.int32) + c
+        at_0 = jnp.full((every, every), 0, jnp.int32) + c
+        line = iota((1, every), 1)
         for which in range(2):
             real, imag = nmat[which, 0], nmat[which, 1]
-            row_r = nmat[which, 0, pl.ds(c, 1), :]
-            row_i = nmat[which, 1, pl.ds(c, 1), :]
-            col_r = jnp.take_along_axis(real, at, axis=1)
-            col_i = jnp.take_along_axis(imag, at, axis=1)
-            pivot = jnp.sum(jnp.where(lane[:1] == c, row_r, 0.0), axis=1, keepdims=True)
-            scale = 1.0 / pivot
-            row_r = jnp.where(lane[:1] == c, 1.0, row_r) * scale
-            row_i = jnp.where(lane[:1] == c, 0.0, row_i) * scale
-            real = jnp.where(on_lane, 0.0, real) - (col_r * row_r - col_i * row_i)
-            imag = jnp.where(on_lane, 0.0, imag) - (col_r * row_i + col_i * row_r)
-            nmat[which, 0] = jnp.where(on_row, row_r, real)
-            nmat[which, 1] = jnp.where(on_row, row_i, imag)
+            row_r = [nmat[which, 0, pl.ds(c + k, 1), :] for k in range(2)]
+            row_i = [nmat[which, 1, pl.ds(c + k, 1), :] for k in range(2)]
+
+            def element(row, k):
+                return jnp.sum(jnp.where(line == c + k, row, 0.0), axis=1, keepdims=True)
+
+            first, last = element(row_r[0], 0), element(row_r[1], 1)
+            across_r, across_i = element(row_r[0], 1), element(row_i[0], 1)
+            scale = 1.0 / (first * last - across_r * across_r - across_i * across_i)
+            first, last = first * scale, last * scale
+            across_r, across_i = across_r * scale, across_i * scale
+            row_r = [jnp.where((line == c) | (line == c + 1), jnp.where(line == c + k, 1.0, 0.0), row_r[k]) for k in range(2)]
+            row_i = [jnp.where((line == c) | (line == c + 1), 0.0, row_i[k]) for k in range(2)]
+            new_r = [
+                last * row_r[0] - across_r * row_r[1] + across_i * row_i[1],
+                first * row_r[1] - across_r * row_r[0] - across_i * row_i[0],
+            ]
+            new_i = [
+                last * row_i[0] - across_r * row_i[1] - across_i * row_r[1],
+                first * row_i[1] - across_r * row_i[0] + across_i * row_r[0],
+            ]
+            on = (lane == c) | (lane == c + 1)
+            sum_r, sum_i = jnp.where(on, 0.0, real), jnp.where(on, 0.0, imag)
+            for k in range(2):
+                col_r = jnp.take_along_axis(real, at_0 + k, axis=1)
+                col_i = jnp.take_along_axis(imag, at_0 + k, axis=1)
+                sum_r = sum_r - (col_r * new_r[k] - col_i * new_i[k])
+                sum_i = sum_i - (col_r * new_i[k] + col_i * new_r[k])
+            nmat[which, 0] = sum_r
+            nmat[which, 1] = sum_i
+            for k in range(2):
+                nmat[which, 0, pl.ds(c + k, 1), :] = new_r[k]
+                nmat[which, 1, pl.ds(c + k, 1), :] = new_i[k]
         return carry
 
-    lax.fori_loop(0, every, eliminate, 0)
+    lax.fori_loop(0, every // 2, eliminate, 0)
 
     for which in range(2):
-        real, imag = margin_full(which, 0), margin_full(which, 1)
         mine = pl.ds(pl.multiple_of(mx * bands, TILE), bands)
-        nr, ni = nmat[which, 0, mine, :], nmat[which, 1, mine, :]
-        zr = exact(nr, real) + exact(ni, imag)
-        zi = exact(ni, real) - exact(nr, imag)
+        qr, qi = qt[which, 0, mine, :], qt[which, 1, mine, :]
+        nr, ni = nmat[which, 0], nmat[which, 1]
+        zr = exact(qr, nr) + exact(qi, ni)
+        zi = exact(qr, ni) - exact(qi, nr)
         both = pltpu.roll(jnp.concatenate([zr, zi], 0), lax.rem((nx - mx) * bands, every), 1)
         zmat[:, which * every : (which + 1) * every] = both if which == 0 else -both
 
+    to_right[3].wait_recv()
+    to_left[3].wait_recv()
+    far_f.wait_recv()
+    far_b.wait_recv()
     coeff = zmat[...]
     for r in range(4):
         rows = slice(r * bands, (r + 1) * bands)
@@ -296,8 +391,8 @@
         mixed = exact(coeff, jnp.concatenate(blocks, 0))
         dr = (mixed[:bands, :half] - mixed[bands:, half:]) / (2.0 * string_step)
         di = (mixed[:bands, half:] + mixed[bands:, :half]) / (2.0 * string_step)
-        der_ref[rows, :half] = dr
-        der_ref[rows, half:] = di
+        der_raw[:, 0, r, :] = dr
+        der_raw[:, 1, r, :] = di
         vec[rows, :half] = -dr
         vec[rows, half:] = -di
 
@@ -358,7 +453,7 @@
     owners_tell(crs, cfull, cr.at[0], cs.at[1], cr.at[1])
     field = fields(recvb, 0)
     field_ref[...] = field
-    pot = jnp.concatenate([pot_ref[...]] * 2, 0)
+    pot = jnp.concatenate([pots_ref[...]] * 2, 0)
     weighted = field * pot
     energy = jnp.sum(weighted * field, axis=0, keepdims=True)
     sendc[...] = triple((t3h_ref[...], t3l_ref[...]), halves(weighted)).reshape(sendc.shape)
@@ -413,7 +508,7 @@
         scal2[...] = scal2[...] + as_row(with_mine, first) + as_row(with_old, first + bands)
 
     field2 = fields(recve, 2)
-    weighted2 = field2 * jnp.concatenate([pot_ref[...]] * 2, 0)
+    weighted2 = field2 * jnp.concatenate([pots_ref[...]] * 2, 0)
     own2 = jnp.sum(weighted2 * field2, axis=0, keepdims=True)
     cross2 = jnp.sum(weighted2 * field_ref[...], axis=0, keepdims=True)
     scal2[...] = scal2[...] + lanes_per_band(own2, 0) + lanes_per_band(cross2, bands)
@@ -427,9 +522,14 @@
         as_column(totals2, 0) + 2.0 * beta * as_column(totals2, bands) + beta * beta * curvature
     )
     alpha2 = norm_next / curvature2
-    sol_ref[...] = down_rows(alpha + alpha2 * beta) * vec[...] + down_rows(alpha2) * res[...]
-
-    for copy in to_right + to_left + [far_right, far_left]:
+    of_first = alpha + alpha2 * beta
+    for r in range(4):
+        rows = slice(r * bands, (r + 1) * bands)
+        total = of_first * vec[rows, :] + alpha2 * res[rows, :]
+        for part in range(2):
+            sol_raw[:, part, r, :] = total[:, part * half : (part + 1) * half]
+
+    for copy in to_right + to_left + [far_right, far_left, far_f, far_b]:
         copy.wait_send()
     across.wait_send()
     sent_to_owners(mpart, ms.at[0])
@@ -462,13 +562,7 @@
     cosine, sine = np.cos(angle) / math.sqrt(length), np.sin(angle) / math.sqrt(length)
     out = np.block([[cosine, -sine], [sine, cosine]])
     order = np.arange(2 * length).reshape(2, peers, length // peers).transpose(1, 0, 2).reshape(-1)
-    first, third = out[order], out.T[order]
-    return (*split_table(first), *split_table(third.T.copy()), *split_table(third))
-
-
-def flat(array):
-    items, parts, rows, width = array.shape
-    return array.transpose(2, 0, 1, 3).reshape(rows * items, parts * width)
+    return split_table(out[order])
 
 
 def body(n, nx, waves, forward, backward, projectors, potential, strengths, shifts):
@@ -477,14 +571,6 @@
     points = float(length * width)
     every = nx * bands
     count = projectors.shape[0]
-    first_index = lax.axis_index("pw") * rows + jnp.arange(rows, dtype=jnp.int32)
-    second_index = jnp.arange(width, dtype=jnp.int32)
-    first_freq, second_freq = centred(first_index, length), centred(second_index, width)
-    kinetic = kinetic_scale * (
-        first_freq[:, None] * first_freq[:, None] + second_freq[None, :] * second_freq[None, :]
-    )
-    diag = (kinetic[:, None, :] + shifts[None, :, None]).reshape(rows * bands, width)
-    pot = jnp.repeat(potential.T, bands, axis=1)
     shape = (rows * bands, parts * width)
     f32 = functools.partial(pltpu.VMEM, dtype=jnp.float32)
     full, tiles = (n, TILE, LANES), 2 * bands // TILE
@@ -492,12 +578,15 @@
     dma = pltpu.SemaphoreType.DMA
     der, sol = pl.pallas_call(
         functools.partial(kernel, n, nx, points),
-        out_shape=[jax.ShapeDtypeStruct(shape, jnp.float32)] * 2,
-        in_specs=[vmem] * 13,
+        out_shape=[jax.ShapeDtypeStruct(waves.shape, jnp.float32)] * 2,
+        in_specs=[vmem] * 9,
         out_specs=[vmem] * 2,
         scratch_shapes=[
-            pltpu.VMEM((rows * count, parts * width), jnp.bfloat16),
-            pltpu.VMEM((rows * count, parts * width), jnp.bfloat16),
+            f32(shape), f32(shape), f32(shape),
+            f32((rows * bands, width)), f32((length, LANES)),
+            *[pltpu.VMEM((rows * count, parts * width), jnp.bfloat16)] * 2,
+            *[pltpu.VMEM((2 * length, 2 * length), jnp.bfloat16)] * 4,
+            f32((nx, *shape)), f32((2, 2, every, every)),
             f32((nx, 2, *shape)),
             f32((2 * tiles, TILE, LANES)), f32(full), f32((2 * tiles, TILE, LANES)),
             f32((nx, 2 * tiles, TILE, LANES)), f32((2, 2, every, every)), f32((2 * bands, 2 * every)),
@@ -507,20 +596,18 @@
             f32((tiles, TILE, LANES)), f32(full),
             f32((1, LANES)), f32((n, 1, LANES)), f32((1, LANES)), f32((n, 1, LANES)),
             f32((n * TILE, LANES)),
-            dma((6,)), dma((6,)), dma((3,)), dma((3,)), dma((3,)), dma((3,)), dma((5,)), dma((5,)),
+            pltpu.SemaphoreType.REGULAR((n.bit_length(),)),
+            dma((12,)), dma((12,)), dma((3,)), dma((3,)), dma((3,)), dma((3,)), dma((5,)), dma((5,)),
         ],
         compiler_params=pltpu.CompilerParams(
             collective_id=0, has_side_effects=True, vmem_limit_bytes=60 * 1024 * 1024
         ),
     )(
-        flat(waves), flat(forward), flat(backward), flat(projectors), diag, pot,
+        waves, forward, backward, projectors, jnp.tile(shifts, rows).reshape(-1, 1), potential,
         strengths.reshape(1, count), *[jnp.asarray(t) for t in tables(length, n)],
     )
 
-    def unflat(array):
-        return array.reshape(rows, bands, parts, width).transpose(1, 2, 0, 3)
-
-    return unflat(sol), unflat(der)
+    return sol, der
 
 
 def solution(mesh):

time: 279 us -> 247 us (0.89)
  Pallas kernels: 267 us -> 242 us
  local copies, waits for them, and re-layouts: 9.9 us -> 3.81 us
    pallas_call x1, Pallas kernels: 267 us -> 242 us  [body(): pl.pallas_call(functools.partial(kernel, n, nx, points), out_shape=[jax.S...]
    transpose x5 -> x0, local copies, waits for them, and re-layouts: 3.3 us -> none  [the longest x4 2.17 us: flat(): return array.transpose(2, 0, 1, 3).reshape(rows * items, parts * width)]
where the time goes in v2:
time: 247 us; the launch traced here: 246 us
  Pallas kernels  242 us (98%)
  local copies, waits for them, and re-layouts  3.81 us (2%)
    pallas_call x1, Pallas kernels, body(): pl.pallas_call(functools.partial(kernel, n, nx, points), out_shape=[jax.S...  242 us

profile of v2, /device:TPU:33, one launch (start us, length us, event | category | flops | bytes accessed | tf_op | source)
XLA Modules:
  0.0 246.3 jit_solution(13495342864439269844)
XLA Ops:
  0.6 0.0 copy-start.1
  0.6 0.6 copy-done.1
  1.3 0.7 reshape_tile.4.shift_ref
  2.0 241.8 %shard_map.104 = (f32[32,2,4,256]{3,2,1,0:T(4,128)}, f32[32,2,4,256]{3,2,1,0:T(4,128)}) custom-call(f32[32,2,4,256]{3,2,1,0:T(4,128)} %w_raw.1, f32[32,2,4,256]{3,2,1,0:T(4,128)} %f_raw.1, f32[32,2,4,256]{3,2,1,0:T(4,128)} %b_raw.1, f32[128,2,4,256]{3,2,1,0:T(4,128)} %p_ref.1, f32[128,1]{1,0:T(8,128)} %reshape_tile.4.shift_ref, f32[4,256]{1,0:T(4,128)} %pot_ref.1, ...), custom_call_target="tpu_custom_call" | custom-call | tf_op jit(solution)/shard_map/pallas_call | solution.py:579
  243.9 0.0 copy-start
  243.9 1.7 copy.14
  245.6 0.0 copy-done
  245.6 0.7 copy.15
  (1 shorter events, 0.0 us)
Async XLA Ops:
  0.6 0.7 copy-start.1
  243.9 1.7 copy-start

commit v3 on v2

--- a/solution.py
+++ b/solution.py
@@ -63,12 +63,12 @@
     t2h_ref, t2l_ref,
     der_raw, sol_raw,
     w_ref, f_ref, b_ref,
-    diag_ref, pots_ref, ph_ref, pl_ref, t1h_ref, t1l_ref, t3h_ref, t3l_ref, wide, qt, near, mpart, mrs, mfull, mall, nmat, zmat,
+    diag_ref, pots_ref, ph_ref, pl_ref, t1h_ref, t1l_ref, t3h_ref, t3l_ref, wide, qt, near, mpart, mpair, msum, mrs, mfull, mall, nmat, zmat,
     vec, res, img,
     sendb, recvb, sendc, recvc, sende, recve,
-    cpart, crs, cfull, cpart2, crs2,
-    scal, scals, scal2, scals2, field_ref,
-    known, xs, xr, ms, mr, cs, cr, es, er,
+    cpart, cpair, csum, crs, cfull, cpart2, cpair2, csum2, crs2,
+    scal, spair, scals, scal2, spair2, scals2, field_ref,
+    known, xs, xr, zs, zr_sem, ms, mr, mm, cm, cm2, sm, sm2, es, er,
 ):
     me = lax.axis_index("pw")
     mx = lax.axis_index("band")
@@ -90,6 +90,8 @@
 
     barrier = pltpu.get_barrier_semaphore()
 
+    partner = me + 1 - 2 * lax.rem(me, 2)
+
     def at_distance(d):
         return lax.rem(me + d + n, n)
 
@@ -97,7 +99,6 @@
         target = at_distance(d) if base is None else base
         pl.semaphore_signal(barrier, inc=1, device_id={axis: target}, device_id_type=MESH)
 
-    partner = me + 1 - 2 * lax.rem(me, 2)
     greet(0, "pw", partner)
     greet(2)
     greet(-2)
@@ -140,78 +141,119 @@
         dst[pl.ds(me, 1)] = src[pl.ds(me, 1)]
         to_others(lambda t: remote(src.at[t], dst.at[me], send, recv, "pw", t).start())
 
-    def tell(src, dst, send, recv):
-        to_others(lambda t: remote(src, dst, send, recv, "pw", t).start())
+    core, place, chips = lax.rem(me, 2), me // 2, n // 2
+
+    def line_other(i):
+        part = (i + 1) // 2
+        chip = lax.rem(place + chips // 2 + part * (2 * lax.rem(i, 2) - 1) + chips, chips)
+        return 2 * chip + core
+
+    def tell_line(src, dst, send, recv):
+        def one(i, carry):
+            remote(src, dst, send, recv, "pw", line_other(i)).start()
+            return carry
+
+        lax.fori_loop(0, chips - 1, one, 0)
 
     def arrived(dst, count, recv):
         some = dst.at[pl.ds(0, count)]
-        remote(some, some, recv, recv, "pw", other(0)).wait_recv()
+        remote(some, some, recv, recv, "pw", partner).wait_recv()
 
     def left_here(src, count, send):
         some = src.at[pl.ds(0, count)]
-        remote(some, some, send, send, "pw", other(0)).wait_send()
-
-    def to_owners(src, dst, send, recv):
-        tiles = src.shape[0]
-        stride = n // tiles
+        remote(some, some, send, send, "pw", partner).wait_send()
+
+    def owner_of(tiles):
+        stride = chips // (tiles // 2)
+        return lax.rem(place, stride) == 0, core * (tiles // 2) + place // stride
+
+    def to_owners(part, pair, summed_pair, dst, sem):
+        tiles = part.shape[0] // 2
+        stride = chips // tiles
+        theirs = pl.ds((1 - core) * tiles, tiles)
+        copy = remote(part.at[theirs], pair, sem.at[0], sem.at[1], "pw", partner)
+        copy.start()
+        copy.wait_recv()
+        summed_pair[...] = part[pl.ds(core * tiles, tiles)] + pair[...]
 
         def one(i, carry):
-            t = lax.rem(i + me // stride, tiles)
-            owner = t * stride
+            t = lax.rem(i + place // stride, tiles)
+            owner = 2 * t * stride + core
 
             @pl.when(owner != me)
             def _():
-                remote(src.at[t], dst.at[me], send, recv, "pw", owner).start()
+                remote(
+                    summed_pair.at[t], dst.at[place], sem.at[2], sem.at[3], "pw", owner
+                ).start()
 
             @pl.when(owner == me)
             def _():
-                dst[pl.ds(me, 1)] = src[pl.ds(t, 1)]
+                dst[pl.ds(place, 1)] = summed_pair[pl.ds(t, 1)]
 
             return carry
 
         lax.fori_loop(0, tiles, one, 0)
 
-    def sent_to_owners(src, send):
-        tiles = src.shape[0]
-        owns = lax.rem(me, n // tiles) == 0
+    def sent_to_owners(part, summed_pair, sem):
+        tiles = summed_pair.shape[0]
+        owns, _ = owner_of(2 * tiles)
+        left_here(part, tiles, sem.at[0])
 
         @pl.when(owns)
         def _():
-            left_here(src, tiles - 1, send)
+            left_here(summed_pair, tiles - 1, sem.at[2])
 
         @pl.when(jnp.logical_not(owns))
         def _():
-            left_here(src, tiles, send)
-
-    def owners_tell(buf, full, recv, tell_send, tell_recv):
-        tiles = full.shape[0]
-        stride = n // tiles
-
-        @pl.when(lax.rem(me, stride) == 0)
-        def _():
-            arrived(buf, n - 1, recv)
-            t = me // stride
-            full[pl.ds(t, 1)] = jnp.sum(buf[...], axis=0, keepdims=True)
-            tell(full.at[t], full.at[t], tell_send, tell_recv)
-
-    def told(full, recv):
-        tiles = full.shape[0]
-        owns = lax.rem(me, n // tiles) == 0
+            left_here(summed_pair, tiles, sem.at[2])
+
+    def owners_tell(buf, full, sem):
+        owns, t = owner_of(full.shape[0])
 
         @pl.when(owns)
         def _():
-            arrived(full, tiles - 1, recv)
+            arrived(buf, chips - 1, sem.at[3])
+            full[pl.ds(t, 1)] = jnp.sum(buf[...], axis=0, keepdims=True)
+            tell_line(full.at[t], full.at[t], sem.at[4], sem.at[5])
+
+    def told(full, sem):
+        tiles = full.shape[0] // 2
+        owns, _ = owner_of(2 * tiles)
+
+        @pl.when(owns)
+        def _():
+            arrived(full, tiles - 1, sem.at[5])
 
         @pl.when(jnp.logical_not(owns))
         def _():
-            arrived(full, tiles, recv)
-
-    def owners_done(buf, full, send):
-        tiles = full.shape[0]
-
-        @pl.when(lax.rem(me, n // tiles) == 0)
+            arrived(full, tiles, sem.at[5])
+
+        mine = full.at[pl.ds(core * tiles, tiles)]
+        remote(mine, mine, sem.at[6], sem.at[7], "pw", partner).start()
+        arrived(full, tiles, sem.at[7])
+
+    def owners_done(buf, full, sem):
+        owns, _ = owner_of(full.shape[0])
+        left_here(full, full.shape[0] // 2, sem.at[6])
+
+        @pl.when(owns)
         def _():
-            left_here(buf, n - 1, send)
+            left_here(buf, chips - 1, sem.at[4])
+
+    def add_up(mine, pair, rows, sem):
+        remote(mine.at[0], pair, sem.at[0], sem.at[1], "pw", partner).start()
+        remote(mine.at[0], pair, sem.at[0], sem.at[1], "pw", partner).wait_recv()
+        mine[1] = mine[0] + pair[...]
+        tell_line(mine.at[1], rows.at[place], sem.at[2], sem.at[3])
+        rows[pl.ds(place, 1)] = mine[1][None]
+
+    def added_up(rows, sem):
+        arrived(rows, chips - 1, sem.at[3])
+        return jnp.sum(rows[...], axis=0)
+
+    def adding_done(mine, rows, sem):
+        remote(mine.at[0], mine.at[0], sem.at[0], sem.at[0], "pw", partner).wait_send()
+        left_here(rows, chips - 1, sem.at[2])
 
     part_rows = w_ref.shape[0] // 2
     lower, upper = pl.ds(0, part_rows), pl.ds(part_rows, part_rows)
@@ -253,7 +295,7 @@
         for r in range(4):
             term = triple(own[r], halves(wide[slot, r * bands : (r + 1) * bands, :]), NT)
             total = term if total is None else total + term
-        nmat[0, 0, :, slot * bands : (slot + 1) * bands] = total
+        nmat[0, :, slot * bands : (slot + 1) * bands] = total
 
     to_right[0].wait_recv()
     far_right = over_band(wide.at[3, lower], wide.at[2, lower], 4, right)
@@ -273,10 +315,10 @@
     far_right.wait_recv()
     far_left.wait_recv()
     margin_of(2)
-    turned = pltpu.roll(nmat[0, 0], mx * bands, 1)
+    turned = pltpu.roll(nmat[0], mx * bands, 1)
     mpart[...] = turned.reshape(mpart.shape)
 
-    to_owners(mpart, mrs, ms.at[0], mr.at[0])
+    to_owners(mpart, mpair, msum, mrs, mm)
     for r in range(4):
         for part in range(2):
             rows = slice(r * every, (r + 1) * every)
@@ -298,93 +340,135 @@
     inverse_table = (t2h_ref[...].astype(jnp.float32) + t2l_ref[...].astype(jnp.float32)) * flip
     t3h_ref[...], t3l_ref[...] = halves(inverse_table)
     t1h_ref[...], t1l_ref[...] = halves(inverse_table.T)
-    owners_tell(mrs, mfull, mr.at[0], ms.at[1], mr.at[1])
+    owners_tell(mrs, mfull, mm)
     to_right[2].wait_recv()
     far_f = over_band(near.at[3, 0], near.at[2, 0], 10, right)
     far_f.start()
     to_left[2].wait_recv()
     far_b = over_band(near.at[1, 1], near.at[2, 1], 11, left)
     far_b.start()
-    told(mfull, mr.at[1])
+    told(mfull, mm)
     mall[pl.ds(mx, 1)] = mfull[...][None]
     for step in range(1, nx):
         t = lax.rem(mx + step, nx)
-        remote(mfull, mall.at[mx], ms.at[2], mr.at[2], "band", t).start()
+        remote(mfull, mall.at[mx], ms, mr, "band", t).start()
     some = mall.at[pl.ds(0, nx - 1)]
-    across = remote(some, some, ms.at[2], mr.at[2], "band", right)
+    across = remote(some, some, ms, mr, "band", right)
     across.wait_recv()
 
-    def margin_full(which, part):
+    def margin_full(part):
         tiles_each = bands // TILE
-        at = (which * 2 + part) * tiles_each
-        rows = [mall[x, at : at + tiles_each].reshape(bands, every) for x in range(nx)]
+        at = pl.ds((core * 2 + part) * tiles_each, tiles_each)
+        rows = [mall[x, at].reshape(bands, every) for x in range(nx)]
         return jnp.concatenate(rows, 0) / points
 
-    for which in range(2):
-        real, imag = margin_full(which, 0), margin_full(which, 1)
-        nmat[which, 0] = exact(real, real, NT) + exact(imag, imag, NT)
-        nmat[which, 1] = exact(imag, real, NT) - exact(real, imag, NT)
-        qt[which, 0] = real.T
-        qt[which, 1] = imag.T
+    real, imag = margin_full(0), margin_full(1)
+    nmat[0] = exact(real, real, NT) + exact(imag, imag, NT)
+    nmat[1] = exact(imag, real, NT) - exact(real, imag, NT)
+    qt[0] = real.T
+    qt[1] = imag.T
+
+    def times(a, b):
+        return a[0] * b[0] - a[1] * b[1], a[0] * b[1] + a[1] * b[0]
+
+    def minus(a, b):
+        return a[0] - b[0], a[1] - b[1]
+
+    def conj(a):
+        return a[0], -a[1]
+
+    def solver(first, last, across):
+        scale = 1.0 / (first * last - across[0] * across[0] - across[1] * across[1])
+        first, last = first * scale, last * scale
+        across = (across[0] * scale, across[1] * scale)
+
+        def solve(x, y):
+            new_x = minus((last * x[0], last * x[1]), times(across, y))
+            return new_x, minus((first * y[0], first * y[1]), times(conj(across), x))
+
+        return solve
 
     def eliminate(step, carry):
-        c = 2 * step
+        c = 4 * step
         lane = iota((every, every), 1)
         at_0 = jnp.full((every, every), 0, jnp.int32) + c
         line = iota((1, every), 1)
-        for which in range(2):
-            real, imag = nmat[which, 0], nmat[which, 1]
-            row_r = [nmat[which, 0, pl.ds(c + k, 1), :] for k in range(2)]
-            row_i = [nmat[which, 1, pl.ds(c + k, 1), :] for k in range(2)]
-
-            def element(row, k):
-                return jnp.sum(jnp.where(line == c + k, row, 0.0), axis=1, keepdims=True)
-
-            first, last = element(row_r[0], 0), element(row_r[1], 1)
-            across_r, across_i = element(row_r[0], 1), element(row_i[0], 1)
-            scale = 1.0 / (first * last - across_r * across_r - across_i * across_i)
-            first, last = first * scale, last * scale
-            across_r, across_i = across_r * scale, across_i * scale
-            row_r = [jnp.where((line == c) | (line == c + 1), jnp.where(line == c + k, 1.0, 0.0), row_r[k]) for k in range(2)]
-            row_i = [jnp.where((line == c) | (line == c + 1), 0.0, row_i[k]) for k in range(2)]
-            new_r = [
-                last * row_r[0] - across_r * row_r[1] + across_i * row_i[1],
-                first * row_r[1] - across_r * row_r[0] - across_i * row_i[0],
-            ]
-            new_i = [
-                last * row_i[0] - across_r * row_i[1] - across_i * row_r[1],
-                first * row_i[1] - across_r * row_i[0] + across_i * row_r[0],
-            ]
-            on = (lane == c) | (lane == c + 1)
-            sum_r, sum_i = jnp.where(on, 0.0, real), jnp.where(on, 0.0, imag)
-            for k in range(2):
-                col_r = jnp.take_along_axis(real, at_0 + k, axis=1)
-                col_i = jnp.take_along_axis(imag, at_0 + k, axis=1)
-                sum_r = sum_r - (col_r * new_r[k] - col_i * new_i[k])
-                sum_i = sum_i - (col_r * new_i[k] + col_i * new_r[k])
-            nmat[which, 0] = sum_r
-            nmat[which, 1] = sum_i
-            for k in range(2):
-                nmat[which, 0, pl.ds(c + k, 1), :] = new_r[k]
-                nmat[which, 1, pl.ds(c + k, 1), :] = new_i[k]
+        lows, highs = (line == c) | (line == c + 1), (line == c + 2) | (line == c + 3)
+        on = (lane >= c) & (lane < c + 4)
+
+        def without(row, where):
+            return jnp.where(where, 0.0, row[0]), jnp.where(where, 0.0, row[1])
+
+        def unit(row, where, k):
+            return jnp.where(where, jnp.where(line == c + k, 1.0, 0.0), row[0]), jnp.where(where, 0.0, row[1])
+
+        real, imag = nmat[0], nmat[1]
+        rows = [
+            (nmat[0, pl.ds(c + k, 1), :], nmat[1, pl.ds(c + k, 1), :])
+            for k in range(4)
+        ]
+
+        def one(row, k):
+            return jnp.sum(jnp.where(line == c + k, row, 0.0), axis=1, keepdims=True)
+
+        def element(j, k):
+            return one(rows[j][0], k), one(rows[j][1], k)
+
+        diag4 = [one(rows[k][0], k) for k in range(4)]
+        off = {(j, k): element(j, k) for j in range(4) for k in range(j + 1, 4)}
+        solve = solver(diag4[0], diag4[1], off[0, 1])
+        head = {k: solve(off[0, k], off[1, k]) for k in (2, 3)}
+
+        def rest(j, k, value):
+            value = minus(value, times(conj(off[0, j]), head[k][0]))
+            return minus(value, times(conj(off[1, j]), head[k][1]))
+
+        zero = jnp.zeros_like(diag4[2])
+        last_solve = solver(
+            rest(2, 2, (diag4[2], zero))[0], rest(3, 3, (diag4[3], zero))[0], rest(2, 3, off[2, 3])
+        )
+        new = list(solve(unit(rows[0], lows, 0), unit(rows[1], lows, 1)))
+        tail = []
+        for k in (2, 3):
+            row = minus(without(rows[k], lows), times(conj(off[0, k]), new[0]))
+            row = minus(row, times(conj(off[1, k]), new[1]))
+            tail.append(unit(row, highs, k))
+        tail = last_solve(*tail)
+        for k in range(2):
+            row = minus(without(new[k], highs), times(head[2][k], tail[0]))
+            new[k] = minus(row, times(head[3][k], tail[1]))
+        new += tail
+        total = jnp.where(on, 0.0, real), jnp.where(on, 0.0, imag)
+        for k in range(4):
+            column = (
+                jnp.take_along_axis(real, at_0 + k, axis=1),
+                jnp.take_along_axis(imag, at_0 + k, axis=1),
+            )
+            total = minus(total, times(column, new[k]))
+        nmat[0], nmat[1] = total
+        for k in range(4):
+            nmat[0, pl.ds(c + k, 1), :] = new[k][0]
+            nmat[1, pl.ds(c + k, 1), :] = new[k][1]
         return carry
 
-    lax.fori_loop(0, every // 2, eliminate, 0)
-
-    for which in range(2):
-        mine = pl.ds(pl.multiple_of(mx * bands, TILE), bands)
-        qr, qi = qt[which, 0, mine, :], qt[which, 1, mine, :]
-        nr, ni = nmat[which, 0], nmat[which, 1]
-        zr = exact(qr, nr) + exact(qi, ni)
-        zi = exact(qr, ni) - exact(qi, nr)
-        both = pltpu.roll(jnp.concatenate([zr, zi], 0), lax.rem((nx - mx) * bands, every), 1)
-        zmat[:, which * every : (which + 1) * every] = both if which == 0 else -both
+    lax.fori_loop(0, every // 4, eliminate, 0)
+
+    mine = pl.ds(pl.multiple_of(mx * bands, TILE), bands)
+    qr, qi = qt[0, mine, :], qt[1, mine, :]
+    nr, ni = nmat[0], nmat[1]
+    zr = exact(qr, nr) + exact(qi, ni)
+    zi = exact(qr, ni) - exact(qi, nr)
+    both = pltpu.roll(jnp.concatenate([zr, zi], 0), lax.rem((nx - mx) * bands, every), 1)
+    zmat[pl.ds(core, 1)] = jnp.where(core == 0, both, -both)[None]
+    swap = remote(zmat.at[core], zmat.at[core], zs, zr_sem, "pw", partner)
+    swap.start()
 
     to_right[3].wait_recv()
     to_left[3].wait_recv()
     far_f.wait_recv()
     far_b.wait_recv()
-    coeff = zmat[...]
+    swap.wait_recv()
+    coeff = jnp.concatenate([zmat[0], zmat[1]], 1)
     for r in range(4):
         rows = slice(r * bands, (r + 1) * bands)
         blocks = [near[d, which, rows, :] for which in range(2) for d in range(nx)]
@@ -407,7 +491,7 @@
         parts = halves(recv[...].reshape(n * TILE, LANES))
         return triple((t1h_ref[...], t1l_ref[...]), parts)
 
-    def project(src, part, buf, send, recv):
+    def project(src, part, pair, summed_pair, buf, sem):
         total = None
         for r in range(4):
             rows = src[r * bands : (r + 1) * bands, :]
@@ -416,7 +500,7 @@
             term = triple(halves(both), (ph_ref[at, :], pl_ref[at, :]), NT)
             total = term if total is None else total + term
         part[...] = (total / points).reshape(part.shape)
-        to_owners(part, buf, send, recv)
+        to_owners(part, pair, summed_pair, buf, sem)
 
     def per_band(values):
         return sum(values[r * bands : (r + 1) * bands] for r in range(1, 4)) + values[:bands]
@@ -447,22 +531,21 @@
     stren = str_ref[...]
 
     forth(vec, sendb, recvb, 0)
-    project(vec, cpart, crs, cs.at[0], cr.at[0])
+    project(vec, cpart, cpair, csum, crs, cm)
     d = vec[...]
     scal_row = as_row(summed(diag * d * d), 0) + as_row(summed(d * d), 2 * bands)
-    owners_tell(crs, cfull, cr.at[0], cs.at[1], cr.at[1])
+    owners_tell(crs, cfull, cm)
     field = fields(recvb, 0)
     field_ref[...] = field
     pot = jnp.concatenate([pots_ref[...]] * 2, 0)
     weighted = field * pot
     energy = jnp.sum(weighted * field, axis=0, keepdims=True)
     sendc[...] = triple((t3h_ref[...], t3l_ref[...]), halves(weighted)).reshape(sendc.shape)
-    scal[...] = scal_row + lanes_per_band(energy, 0)
-    tell(scal, scals.at[me], es.at[3], er.at[3])
     exchange(sendc, recvc, es.at[1], er.at[1])
-    scals[pl.ds(me, 1)] = scal[...][None]
-
-    told(cfull, cr.at[1])
+    scal[0] = scal_row + lanes_per_band(energy, 0)
+    add_up(scal, spair, scals, sm)
+
+    told(cfull, cm)
     coupled = cfull[...].reshape(2 * bands, every)
     weights = halves(coupled * stren)
     for r in range(4):
@@ -473,8 +556,7 @@
         img[rows, half:] = mixed[:bands, half:] + mixed[bands:, :half]
     pair = jnp.sum(stren * coupled * coupled, axis=1, keepdims=True)
     own_pair = points * (pair[:bands] + pair[bands:])
-    arrived(scals, n - 1, er.at[3])
-    totals = jnp.sum(scals[...], axis=0)
+    totals = added_up(scals, sm)
     norm_now = as_column(totals, 2 * bands)
     curvature = as_column(totals, 0) + own_pair
     alpha = norm_now / curvature
@@ -487,35 +569,32 @@
     res[...] = d - down_rows(alpha) * image
 
     forth(res, sende, recve, 2)
-    project(res, cpart2, crs2, cs.at[2], cr.at[2])
+    project(res, cpart2, cpair2, csum2, crs2, cm2)
     d, r2 = vec[...], res[...]
     stiff = diag * r2
     row2 = as_row(summed(stiff * r2), 0) + as_row(summed(stiff * d), bands)
     row2 = row2 + as_row(summed(r2 * r2), 2 * bands)
-    scal2[...] = row2
-    tiles2 = cpart2.shape[0]
-    stride2 = n // tiles2
-
-    @pl.when(lax.rem(me, stride2) == 0)
+    scal2[0] = row2
+    owns2, tile2 = owner_of(cpart2.shape[0])
+
+    @pl.when(owns2)
     def _():
-        arrived(crs2, n - 1, cr.at[2])
-        t = me // stride2
+        arrived(crs2, chips - 1, cm2.at[3])
+        t = tile2
         mine = jnp.sum(crs2[...], axis=0)
         old = cfull[pl.ds(t, 1)].reshape(TILE, every)
         first = lax.rem(t * TILE, bands)
         with_mine = points * jnp.sum(stren * mine * mine, axis=1, keepdims=True)
         with_old = points * jnp.sum(stren * mine * old, axis=1, keepdims=True)
-        scal2[...] = scal2[...] + as_row(with_mine, first) + as_row(with_old, first + bands)
+        scal2[0] = scal2[0] + as_row(with_mine, first) + as_row(with_old, first + bands)
 
     field2 = fields(recve, 2)
     weighted2 = field2 * jnp.concatenate([pots_ref[...]] * 2, 0)
     own2 = jnp.sum(weighted2 * field2, axis=0, keepdims=True)
     cross2 = jnp.sum(weighted2 * field_ref[...], axis=0, keepdims=True)
-    scal2[...] = scal2[...] + lanes_per_band(own2, 0) + lanes_per_band(cross2, bands)
-    tell(scal2, scals2.at[me], es.at[4], er.at[4])
-    scals2[pl.ds(me, 1)] = scal2[...][None]
-    arrived(scals2, n - 1, er.at[4])
-    totals2 = jnp.sum(scals2[...], axis=0)
+    scal2[0] = scal2[0] + lanes_per_band(own2, 0) + lanes_per_band(cross2, bands)
+    add_up(scal2, spair2, scals2, sm2)
+    totals2 = added_up(scals2, sm2)
     norm_next = as_column(totals2, 2 * bands)
     beta = norm_next / norm_now
     curvature2 = (
@@ -532,16 +611,17 @@
     for copy in to_right + to_left + [far_right, far_left, far_f, far_b]:
         copy.wait_send()
     across.wait_send()
-    sent_to_owners(mpart, ms.at[0])
-    owners_done(mrs, mfull, ms.at[1])
-    sent_to_owners(cpart, cs.at[0])
-    owners_done(crs, cfull, cs.at[1])
-    sent_to_owners(cpart2, cs.at[2])
+    swap.wait_send()
+    sent_to_owners(mpart, msum, mm)
+    owners_done(mrs, mfull, mm)
+    sent_to_owners(cpart, csum, cm)
+    owners_done(crs, cfull, cm)
+    sent_to_owners(cpart2, csum2, cm2)
     left_here(sendb, n - 1, es.at[0])
     left_here(sendc, n - 1, es.at[1])
     left_here(sende, n - 1, es.at[2])
-    left_here(scals, n - 1, es.at[3])
-    left_here(scals2, n - 1, es.at[4])
+    adding_done(scal, scals, sm)
+    adding_done(scal2, scals2, sm2)
 
 
 def centred(index, length):
@@ -573,7 +653,7 @@
     count = projectors.shape[0]
     shape = (rows * bands, parts * width)
     f32 = functools.partial(pltpu.VMEM, dtype=jnp.float32)
-    full, tiles = (n, TILE, LANES), 2 * bands // TILE
+    full, line, tiles = (n, TILE, LANES), (n // 2, TILE, LANES), 2 * bands // TILE
     vmem = pl.BlockSpec(memory_space=pltpu.VMEM)
     dma = pltpu.SemaphoreType.DMA
     der, sol = pl.pallas_call(
@@ -586,18 +666,21 @@
             f32((rows * bands, width)), f32((length, LANES)),
             *[pltpu.VMEM((rows * count, parts * width), jnp.bfloat16)] * 2,
             *[pltpu.VMEM((2 * length, 2 * length), jnp.bfloat16)] * 4,
-            f32((nx, *shape)), f32((2, 2, every, every)),
+            f32((nx, *shape)), f32((2, every, every)),
             f32((nx, 2, *shape)),
-            f32((2 * tiles, TILE, LANES)), f32(full), f32((2 * tiles, TILE, LANES)),
-            f32((nx, 2 * tiles, TILE, LANES)), f32((2, 2, every, every)), f32((2 * bands, 2 * every)),
+            f32((2 * tiles, TILE, LANES)), *[f32((tiles, TILE, LANES))] * 2, f32(line),
+            f32((2 * tiles, TILE, LANES)),
+            f32((nx, 2 * tiles, TILE, LANES)), f32((2, every, every)), f32((2, 2 * bands, every)),
             f32(shape), f32(shape), f32(shape),
             f32(full), f32(full), f32(full), f32(full), f32(full), f32(full),
-            f32((tiles, TILE, LANES)), f32(full), f32((tiles, TILE, LANES)),
-            f32((tiles, TILE, LANES)), f32(full),
-            f32((1, LANES)), f32((n, 1, LANES)), f32((1, LANES)), f32((n, 1, LANES)),
+            f32((tiles, TILE, LANES)), *[f32((tiles // 2, TILE, LANES))] * 2, f32(line),
+            f32((tiles, TILE, LANES)),
+            f32((tiles, TILE, LANES)), *[f32((tiles // 2, TILE, LANES))] * 2, f32(line),
+            *[f32((2, 1, LANES)), f32((1, LANES)), f32((n // 2, 1, LANES))] * 2,
             f32((n * TILE, LANES)),
             pltpu.SemaphoreType.REGULAR((n.bit_length(),)),
-            dma((12,)), dma((12,)), dma((3,)), dma((3,)), dma((3,)), dma((3,)), dma((5,)), dma((5,)),
+            dma((12,)), dma((12,)), dma, dma, dma, dma, dma((8,)), dma((8,)), dma((8,)), dma((4,)), dma((4,)),
+            dma((3,)), dma((3,)),
         ],
         compiler_params=pltpu.CompilerParams(
             collective_id=0, has_side_effects=True, vmem_limit_bytes=60 * 1024 * 1024

time: 247 us -> 232 us (0.939)
  Pallas kernels: 242 us -> 228 us
    pallas_call x1, Pallas kernels: 242 us -> 228 us  [body(): pl.pallas_call(functools.partial(kernel, n, nx, points), out_shape=[jax.S...]
where the time goes in v3:
time: 232 us
  Pallas kernels  228 us (98%)
  local copies, waits for them, and re-layouts  3.81 us (2%)
    pallas_call x1, Pallas kernels, body(): pl.pallas_call(functools.partial(kernel, n, nx, points), out_shape=[jax.S...  228 us

profile of v3, /device:TPU:33, one launch (start us, length us, event | category | flops | bytes accessed | tf_op | source)
XLA Modules:
  0.0 232.3 jit_solution(5957090405991296591)
XLA Ops:
  0.6 0.0 copy-start.1
  0.6 0.6 copy-done.1
  1.3 0.7 reshape_tile.4.shift_ref
  2.0 227.8 %shard_map.104 = (f32[32,2,4,256]{3,2,1,0:T(4,128)}, f32[32,2,4,256]{3,2,1,0:T(4,128)}) custom-call(f32[32,2,4,256]{3,2,1,0:T(4,128)} %w_raw.1, f32[32,2,4,256]{3,2,1,0:T(4,128)} %f_raw.1, f32[32,2,4,256]{3,2,1,0:T(4,128)} %b_raw.1, f32[128,2,4,256]{3,2,1,0:T(4,128)} %p_ref.1, f32[128,1]{1,0:T(8,128)} %reshape_tile.4.shift_ref, f32[4,256]{1,0:T(4,128)} %pot_ref.1, ...), custom_call_target="tpu_custom_call" | custom-call | tf_op jit(solution)/shard_map/pallas_call | solution.py:659
  229.9 0.0 copy-start
  229.9 1.7 copy.14
  231.6 0.0 copy-done
  231.6 0.7 copy.15
  (1 shorter events, 0.0 us)
Async XLA Ops:
  0.6 0.7 copy-start.1
  229.9 1.7 copy-start

commit v4 on v3

--- a/solution.py
+++ b/solution.py
@@ -109,16 +109,24 @@
     flatten(b_raw, b_ref)
     pl.semaphore_wait(barrier, 3 + nx - 1)
 
-    def learn(k):
+    rounds = (n // 4).bit_length() - 1
+
+    def say(k):
         d = 2 << k
         for target in (at_distance(d), at_distance(-d)):
             pl.semaphore_signal(known.at[k], inc=1, device_id={"pw": target}, device_id_type=MESH)
+
+    def hear(k):
         pl.semaphore_wait(known.at[k], 2)
 
-    rounds = (n // 4).bit_length() - 1
-
-    def learn_partner():
+    def learn(k):
+        say(k)
+        hear(k)
+
+    def say_to_partner():
         pl.semaphore_signal(known.at[rounds], inc=1, device_id={"pw": partner}, device_id_type=MESH)
+
+    def hear_partner():
         pl.semaphore_wait(known.at[rounds], 1)
 
     def remote(src, dst, send, recv, axis, target):
@@ -228,13 +236,14 @@
         def _():
             arrived(full, tiles, sem.at[5])
 
+    def told_chip(full, sem):
+        tiles = full.shape[0] // 2
         mine = full.at[pl.ds(core * tiles, tiles)]
         remote(mine, mine, sem.at[6], sem.at[7], "pw", partner).start()
         arrived(full, tiles, sem.at[7])
 
     def owners_done(buf, full, sem):
         owns, _ = owner_of(full.shape[0])
-        left_here(full, full.shape[0] // 2, sem.at[6])
 
         @pl.when(owns)
         def _():
@@ -276,12 +285,12 @@
     for a, b in zip(to_right, to_left):
         a.start()
         b.start()
+    say(0)
     wide[0] = w_ref[...]
     near[0, 0] = f_ref[...]
     near[0, 1] = b_ref[...]
-    learn(0)
-    learn(1)
-
+    hear(0)
+    say(1)
     own = []
     for r in range(4):
         both = []
@@ -297,26 +306,32 @@
             total = term if total is None else total + term
         nmat[0, :, slot * bands : (slot + 1) * bands] = total
 
+    hear(1)
+    say(2)
     to_right[0].wait_recv()
     far_right = over_band(wide.at[3, lower], wide.at[2, lower], 4, right)
     far_right.start()
     to_left[0].wait_recv()
     far_left = over_band(wide.at[1, upper], wide.at[2, upper], 5, left)
     far_left.start()
-    learn(2)
+    hear(2)
+    for k in range(3, rounds - 1):
+        learn(k)
+    if rounds > 3:
+        say(rounds - 1)
     margin_of(0)
     to_right[1].wait_recv()
     margin_of(3)
     to_left[1].wait_recv()
     margin_of(1)
-    for k in range(3, rounds):
-        learn(k)
-    learn_partner()
     far_right.wait_recv()
     far_left.wait_recv()
     margin_of(2)
     turned = pltpu.roll(nmat[0], mx * bands, 1)
     mpart[...] = turned.reshape(mpart.shape)
+    if rounds > 3:
+        hear(rounds - 1)
+    say_to_partner()
 
     to_owners(mpart, mpair, msum, mrs, mm)
     for r in range(4):
@@ -348,17 +363,18 @@
     far_b = over_band(near.at[1, 1], near.at[2, 1], 11, left)
     far_b.start()
     told(mfull, mm)
-    mall[pl.ds(mx, 1)] = mfull[...][None]
+    mine_half = pl.ds(core * (mfull.shape[0] // 2), mfull.shape[0] // 2)
+    mall[pl.ds(mx, 1)] = mfull[mine_half][None]
     for step in range(1, nx):
         t = lax.rem(mx + step, nx)
-        remote(mfull, mall.at[mx], ms, mr, "band", t).start()
+        remote(mfull.at[mine_half], mall.at[mx], ms, mr, "band", t).start()
     some = mall.at[pl.ds(0, nx - 1)]
     across = remote(some, some, ms, mr, "band", right)
     across.wait_recv()
 
     def margin_full(part):
         tiles_each = bands // TILE
-        at = pl.ds((core * 2 + part) * tiles_each, tiles_each)
+        at = slice(part * tiles_each, (part + 1) * tiles_each)
         rows = [mall[x, at].reshape(bands, every) for x in range(nx)]
         return jnp.concatenate(rows, 0) / points
 
@@ -467,6 +483,7 @@
     to_left[3].wait_recv()
     far_f.wait_recv()
     far_b.wait_recv()
+    hear_partner()
     swap.wait_recv()
     coeff = jnp.concatenate([zmat[0], zmat[1]], 1)
     for r in range(4):
@@ -546,6 +563,7 @@
     add_up(scal, spair, scals, sm)
 
     told(cfull, cm)
+    told_chip(cfull, cm)
     coupled = cfull[...].reshape(2 * bands, every)
     weights = halves(coupled * stren)
     for r in range(4):
@@ -616,6 +634,7 @@
     owners_done(mrs, mfull, mm)
     sent_to_owners(cpart, csum, cm)
     owners_done(crs, cfull, cm)
+    left_here(cfull, cfull.shape[0] // 2, cm.at[6])
     sent_to_owners(cpart2, csum2, cm2)
     left_here(sendb, n - 1, es.at[0])
     left_here(sendc, n - 1, es.at[1])
@@ -670,7 +689,7 @@
             f32((nx, 2, *shape)),
             f32((2 * tiles, TILE, LANES)), *[f32((tiles, TILE, LANES))] * 2, f32(line),
             f32((2 * tiles, TILE, LANES)),
-            f32((nx, 2 * tiles, TILE, LANES)), f32((2, every, every)), f32((2, 2 * bands, every)),
+            f32((nx, tiles, TILE, LANES)), f32((2, every, every)), f32((2, 2 * bands, every)),
             f32(shape), f32(shape), f32(shape),
             f32(full), f32(full), f32(full), f32(full), f32(full), f32(full),
             f32((tiles, TILE, LANES)), *[f32((tiles // 2, TILE, LANES))] * 2, f32(line),

time: 232 us -> 230 us (level)
  Pallas kernels: 228 us -> 225 us
    pallas_call x1, Pallas kernels: 228 us -> 225 us  [body(): pl.pallas_call(functools.partial(kernel, n, nx, points), out_shape=[jax.S...]
where the time goes in v4:
time: 230 us
  Pallas kernels  225 us (98%)
  local copies, waits for them, and re-layouts  3.81 us (2%)
    pallas_call x1, Pallas kernels, body(): pl.pallas_call(functools.partial(kernel, n, nx, points), out_shape=[jax.S...  225 us

profile of v4, /device:TPU:33, one launch (start us, length us, event | category | flops | bytes accessed | tf_op | source)
XLA Modules:
  0.0 229.8 jit_solution(7614618206715648421)
XLA Ops:
  0.6 0.0 copy-start.1
  0.6 0.6 copy-done.1
  1.3 0.7 reshape_tile.4.shift_ref
  2.0 225.3 %shard_map.104 = (f32[32,2,4,256]{3,2,1,0:T(4,128)}, f32[32,2,4,256]{3,2,1,0:T(4,128)}) custom-call(f32[32,2,4,256]{3,2,1,0:T(4,128)} %w_raw.1, f32[32,2,4,256]{3,2,1,0:T(4,128)} %f_raw.1, f32[32,2,4,256]{3,2,1,0:T(4,128)} %b_raw.1, f32[128,2,4,256]{3,2,1,0:T(4,128)} %p_ref.1, f32[128,1]{1,0:T(8,128)} %reshape_tile.4.shift_ref, f32[4,256]{1,0:T(4,128)} %pot_ref.1, ...), custom_call_target="tpu_custom_call" | custom-call | tf_op jit(solution)/shard_map/pallas_call | solution.py:678
  227.4 0.0 copy-start
  227.4 1.7 copy.14
  229.1 0.0 copy-done
  229.1 0.7 copy.15
  (1 shorter events, 0.0 us)
Async XLA Ops:
  0.6 0.7 copy-start.1
  227.4 1.7 copy-start

commit v5 on v4

--- a/solution.py
+++ b/solution.py
@@ -175,13 +175,15 @@
         stride = chips // (tiles // 2)
         return lax.rem(place, stride) == 0, core * (tiles // 2) + place // stride
 
+    def to_partner(part, pair, sem):
+        tiles = part.shape[0] // 2
+        theirs = pl.ds((1 - core) * tiles, tiles)
+        return remote(part.at[theirs], pair, sem.at[0], sem.at[1], "pw", partner)
+
     def to_owners(part, pair, summed_pair, dst, sem):
         tiles = part.shape[0] // 2
         stride = chips // tiles
-        theirs = pl.ds((1 - core) * tiles, tiles)
-        copy = remote(part.at[theirs], pair, sem.at[0], sem.at[1], "pw", partner)
-        copy.start()
-        copy.wait_recv()
+        to_partner(part, pair, sem).wait_recv()
         summed_pair[...] = part[pl.ds(core * tiles, tiles)] + pair[...]
 
         def one(i, carry):
@@ -333,6 +335,7 @@
         hear(rounds - 1)
     say_to_partner()
 
+    to_partner(mpart, mpair, mm).start()
     to_owners(mpart, mpair, msum, mrs, mm)
     for r in range(4):
         for part in range(2):
@@ -497,18 +500,17 @@
         vec[rows, :half] = -dr
         vec[rows, half:] = -di
 
-    def forth(src, send, recv, sem):
+    def half_way(src, send):
         parts = halves(src[...])
         out = triple((t2h_ref[...], t2l_ref[...]), parts, NT)
         send[...] = swap_blocks(out.reshape(n, TILE, LANES))
-        exchange(send, recv, es.at[sem], er.at[sem])
 
     def fields(recv, sem):
         arrived(recv, n - 1, er.at[sem])
         parts = halves(recv[...].reshape(n * TILE, LANES))
         return triple((t1h_ref[...], t1l_ref[...]), parts)
 
-    def project(src, part, pair, summed_pair, buf, sem):
+    def project(src, part, pair, sem):
         total = None
         for r in range(4):
             rows = src[r * bands : (r + 1) * bands, :]
@@ -517,7 +519,7 @@
             term = triple(halves(both), (ph_ref[at, :], pl_ref[at, :]), NT)
             total = term if total is None else total + term
         part[...] = (total / points).reshape(part.shape)
-        to_owners(part, pair, summed_pair, buf, sem)
+        to_partner(part, pair, sem).start()
 
     def per_band(values):
         return sum(values[r * bands : (r + 1) * bands] for r in range(1, 4)) + values[:bands]
@@ -547,8 +549,10 @@
     diag = jnp.concatenate([diag_ref[...]] * 2, 1)
     stren = str_ref[...]
 
-    forth(vec, sendb, recvb, 0)
-    project(vec, cpart, cpair, csum, crs, cm)
+    project(vec, cpart, cpair, cm)
+    half_way(vec, sendb)
+    to_owners(cpart, cpair, csum, crs, cm)
+    exchange(sendb, recvb, es.at[0], er.at[0])
     d = vec[...]
     scal_row = as_row(summed(diag * d * d), 0) + as_row(summed(d * d), 2 * bands)
     owners_tell(crs, cfull, cm)
@@ -586,8 +590,10 @@
     image = diag * d + smooth + img[...]
     res[...] = d - down_rows(alpha) * image
 
-    forth(res, sende, recve, 2)
-    project(res, cpart2, cpair2, csum2, crs2, cm2)
+    project(res, cpart2, cpair2, cm2)
+    half_way(res, sende)
+    to_owners(cpart2, cpair2, csum2, crs2, cm2)
+    exchange(sende, recve, es.at[2], er.at[2])
     d, r2 = vec[...], res[...]
     stiff = diag * r2
     row2 = as_row(summed(stiff * r2), 0) + as_row(summed(stiff * d), bands)

time: 230 us -> 227 us (0.987)
  Pallas kernels: 225 us -> 222 us
    pallas_call x1, Pallas kernels: 225 us -> 222 us  [body(): pl.pallas_call(functools.partial(kernel, n, nx, points), out_shape=[jax.S...]
where the time goes in v5:
time: 227 us; the launch traced here: 226 us
  Pallas kernels  222 us (98%)
  local copies, waits for them, and re-layouts  3.81 us (2%)
    pallas_call x1, Pallas kernels, body(): pl.pallas_call(functools.partial(kernel, n, nx, points), out_shape=[jax.S...  222 us

profile of v5, /device:TPU:33, one launch (start us, length us, event | category | flops | bytes accessed | tf_op | source)
XLA Modules:
  0.0 226.3 jit_solution(6524407131750455623)
XLA Ops:
  0.6 0.0 copy-start.1
  0.6 0.6 copy-done.1
  1.3 0.7 reshape_tile.4.shift_ref
  2.0 221.9 %shard_map.104 = (f32[32,2,4,256]{3,2,1,0:T(4,128)}, f32[32,2,4,256]{3,2,1,0:T(4,128)}) custom-call(f32[32,2,4,256]{3,2,1,0:T(4,128)} %w_raw.1, f32[32,2,4,256]{3,2,1,0:T(4,128)} %f_raw.1, f32[32,2,4,256]{3,2,1,0:T(4,128)} %b_raw.1, f32[128,2,4,256]{3,2,1,0:T(4,128)} %p_ref.1, f32[128,1]{1,0:T(8,128)} %reshape_tile.4.shift_ref, f32[4,256]{1,0:T(4,128)} %pot_ref.1, ...), custom_call_target="tpu_custom_call" | custom-call | tf_op jit(solution)/shard_map/pallas_call | solution.py:684
  223.9 0.0 copy-start
  223.9 1.7 copy.14
  225.6 0.0 copy-done
  225.6 0.7 copy.15
  (1 shorter events, 0.0 us)
Async XLA Ops:
  0.6 0.7 copy-start.1
  223.9 1.7 copy-start
